TPU v7x, 128 devices: a whole 4x4x4 slice. The times are simulated.
128 devices in a mesh: blk: 64 (over x, y, z_lo, core), grp: 2 (over z_hi).
Axes of the slice: x: 4, y: 4, z: 4 (z_hi: 2, z_lo: 2; z = z_hi * 2 + z_lo), core: 2. Of those that a mesh axis runs over, the one named last changes fastest.
Arguments:
- sky_maps: float32 [4, 512, 4096], P(None, ('blk', 'grp')), may hold values from -6 to 6
- legendre: bfloat16 [512, 512, 2048], P(('blk', 'grp')), may hold values from -0.25 to 0.25
- owner_table: int32 [512], replicated, may hold values from 0 to 511, each once
Outputs:
- harmonics: float32 [512, 4, 2, 2048], P(('blk', 'grp'))
- spectra: float32 [10, 2048], P(None, ('blk', 'grp'))
Inputs may be any that keep to these rules, and one draw needn't show every extreme that they name: `owner_table`: a permutation of the orders 0 to 511.
All inputs are finite; a program needn't handle non-finite values.
Results may differ from a plain program's by a relative error of at most 0.0034.
Values may be sent and summed in bfloat16 or wider, within the bound.
No kernel may reach another device: no remote copies, remote signals or barrier semaphores. Data moves between devices by JAX's collectives and lax.ppermute only.
A program may use at most 128 MiB of HBM per device.

v0:
```python
import functools
import math

import jax
import jax.numpy as jnp
import numpy as np
from jax import lax
from jax.experimental import pallas as pl
from jax.experimental.pallas import tpu as pltpu
from jax.sharding import Mesh
from jax.sharding import PartitionSpec as P


BLK_GRP = ("blk_0", "blk_1", "blk_2", "blk_3", "grp")
X, Y, Z, CORE = "blk_0", "blk_1", "z", "blk_3"
COLOURS = (
    (0, 768, ((X, Y, Z), (Y, Z, X))),
    (768, 256, ((Z, X, Y), (Z, X, Y))),
)
PIECES = ((0, 384, 0), (384, 384, 0), (768, 256, 1))
SHIFTS = (2, 1, 3)
F32, BF16 = jnp.float32, jnp.bfloat16
SMEM = pl.BlockSpec(memory_space=pltpu.SMEM)
VMEM = pl.BlockSpec(memory_space=pltpu.VMEM)
HBM = pl.BlockSpec(memory_space=pltpu.HBM)


def places(device):
    return {
        X: device // 32,
        Y: device // 8 % 4,
        Z: device % 2 * 2 + device // 4 % 2,
        CORE: device // 2 % 2,
    }


def index_of(place):
    z = place[Z]
    return place[X] * 32 + place[Y] * 8 + z % 2 * 4 + place[CORE] * 2 + z // 2


def shift_along(x, axes, shift):
    pairs = []
    for device in range(128):
        place = places(device)
        axis = axes[place[CORE]]
        pairs.append((device, index_of({**place, axis: (place[axis] + shift) % 4})))
    return lax.ppermute(x, BLK_GRP, pairs)


def swap_cores(x):
    return lax.ppermute(x, CORE, [(0, 1), (1, 0)])


def kernel_call(kernel, mib, flops, **kwargs):
    return pl.pallas_call(
        kernel,
        compiler_params=pltpu.CompilerParams(vmem_limit_bytes=mib << 20),
        cost_estimate=pl.CostEstimate(flops=flops, bytes_accessed=1 << 20, transcendentals=0),
        **kwargs,
    )


def half_copy(first, width, core_ref, leg_ref, out_ref, sem):
    start = pl.multiple_of((1 - core_ref[0]) * 1024 + first, 128)
    return pltpu.make_async_copy(leg_ref.at[:, :, pl.ds(start, width)], out_ref, sem)


def halves_kernel(core_ref, leg_ref, *rest):
    outs, sems = rest[:-1], rest[-1]
    copies = [
        half_copy(first, width, core_ref, leg_ref, out, sems.at[k])
        for k, ((first, width, _), out) in enumerate(zip(PIECES[1:], outs))
    ]
    for copy in copies:
        copy.start()
    for copy in copies:
        copy.wait()


def later_halves(core, legendre):
    return kernel_call(
        halves_kernel,
        48,
        1 << 20,
        out_shape=[jax.ShapeDtypeStruct((4, 512, width), BF16) for _, width, _ in PIECES[1:]],
        in_specs=[SMEM, HBM],
        out_specs=[VMEM] * len(PIECES[1:]),
        scratch_shapes=[pltpu.SemaphoreType.DMA((len(PIECES) - 1,))],
    )(core, legendre)


def real_fft(values):
    n = len(values)
    if n == 1:
        return [(values[0], None)]
    even, odd = real_fft(values[0::2]), real_fft(values[1::2])
    half = n // 2
    out = []
    for k in range(half + 1):
        er, ei = pick(even, k % half, half)
        orr, oi = pick(odd, k % half, half)
        c, s = math.cos(2 * math.pi * k / n), math.sin(2 * math.pi * k / n)
        if k == 0:
            tr, ti = orr, oi
        elif 2 * k == n:
            tr, ti = -orr, (None if oi is None else -oi)
        elif 4 * k == n:
            tr, ti = oi, -orr
        else:
            tr = orr * c if oi is None else orr * c + oi * s
            ti = -orr * s if oi is None else oi * c - orr * s
        out.append((plus(er, tr), plus(ei, ti)))
    return out


def plus(a, b):
    if a is None:
        return b
    return a if b is None else a + b


def pick(spectrum, k, n):
    if k <= n // 2:
        return spectrum[k]
    re, im = spectrum[n - k]
    return re, (None if im is None else -im)


def fourier_kernel(
    first, width, core_ref, leg_ref, sky_ref, waves_ref, out_ref, send_ref, half_ref, x_ref, cos_ref, sin_ref, tail_ref, z_ref, sems
):
    half = half_copy(first, width, core_ref, leg_ref, half_ref, sems.at[0])
    copies = [
        pltpu.make_async_copy(sky_ref, x_ref, sems.at[1]),
        pltpu.make_async_copy(waves_ref.at[0:32], cos_ref, sems.at[2]),
        pltpu.make_async_copy(waves_ref.at[32:64], sin_ref, sems.at[3]),
        pltpu.make_async_copy(waves_ref.at[64:320], tail_ref, sems.at[4]),
    ]
    for copy in copies:
        copy.start()
    half.start()
    for copy in copies:
        copy.wait()
    row = lax.broadcasted_iota(jnp.int32, (8, 128), 0)
    total = None
    for r in range(4):
        slabs = []
        for k in range(32):
            maps = [jnp.broadcast_to(x_ref[a, r : r + 1, 128 * k : 128 * k + 128], (8, 128)) for a in range(4)]
            low, high = jnp.where(row < 2, maps[0], maps[1]), jnp.where(row < 6, maps[2], maps[3])
            slabs.append(jnp.where(row < 4, low, high))
        spectrum = real_fft(slabs)
        for m in range(32):
            re, im = pick(spectrum, m, 32)
            c, s = cos_ref[m : m + 1, :], sin_ref[m : m + 1, :]
            if im is None:
                re, im = re * c, -re * s
            else:
                re, im = re * c + im * s, im * c - re * s
            z_ref[8 * m : 8 * m + 8, 0:128] = jnp.where(row % 2 == 0, re, im)
            z_ref[8 * m : 8 * m + 8, 128:256] = jnp.where(row % 2 == 0, im, -re)
        out = jnp.dot(z_ref[...], tail_ref[...], precision=lax.Precision.HIGHEST, preferred_element_type=F32)
        out = pltpu.roll(out, 16 * r, 1) if r else out
        total = out if total is None else total + out
    rounded = (total * (1.0 / 64.0)).astype(BF16)
    out_ref[...] = rounded
    send_ref[...] = rounded
    half.wait()


def fourier_and_half(first, width, core, legendre, sky_maps):
    turn = 2 * np.pi / 4096 * np.outer(np.arange(32), np.arange(128))
    last = 2 * np.pi / 128 * np.outer(np.arange(128), np.arange(16))
    tail = np.zeros((256, 128))
    tail[:128, :16] = np.cos(last)
    tail[128:, :16] = np.sin(last)
    waves = np.concatenate([np.cos(turn), np.sin(turn), tail])
    return kernel_call(
        functools.partial(fourier_kernel, first, width),
        55,
        width * 8192,
        out_shape=[jax.ShapeDtypeStruct((256, 128), BF16)] * 2 + [jax.ShapeDtypeStruct((4, 512, width), BF16)],
        in_specs=[SMEM] + [HBM] * 3,
        out_specs=[VMEM] * 3,
        scratch_shapes=[
            pltpu.VMEM((4, 4, 4096), F32),
            pltpu.VMEM((32, 128), F32),
            pltpu.VMEM((32, 128), F32),
            pltpu.VMEM((256, 128), F32),
            pltpu.VMEM((256, 256), F32),
            pltpu.SemaphoreType.DMA((5,)),
        ],
    )(core, legendre, sky_maps, jnp.asarray(waves, F32))


def weights_kernel(core_ref, leg_ref, own_ref, got_ref, *rest):
    out_ref, table_ref, sem = rest[-3:]
    start = pl.multiple_of(core_ref[0] * 1024, 128)
    copy = pltpu.make_async_copy(leg_ref.at[:, :, pl.ds(start, 1024)], table_ref, sem)
    copy.start()
    order_weights(own_ref, got_ref, out_ref)
    copy.wait()


def weights_and_own_half(core, legendre, own_f, got_f, *after):
    return kernel_call(
        weights_kernel,
        42,
        1 << 26,
        out_shape=[jax.ShapeDtypeStruct((16, 256, 256), BF16), jax.ShapeDtypeStruct((4, 512, 1024), BF16)],
        in_specs=[SMEM, HBM, VMEM, VMEM] + [HBM] * len(after),
        out_specs=[VMEM] * 2,
        scratch_shapes=[pltpu.SemaphoreType.DMA],
    )(core, legendre, own_f, got_f, *after)


def order_weights(own_ref, got_ref, out_ref):
    columns = jnp.concatenate([own_ref[...], got_ref[...]], axis=1)
    k = lax.broadcasted_iota(jnp.int32, (256, 256), 0)
    n = lax.broadcasted_iota(jnp.int32, (256, 256), 1)
    cycle_of = jnp.where(k % 128 < 64, (k // 128) * 4 + (k % 128) // 16, -1)
    spread = jnp.where(cycle_of == n // 32, 1.0, 0.0).astype(BF16)
    keep = jnp.where((k // 8) == (n % 32), 1.0, 0.0).astype(BF16)
    for g in range(16):
        pick_group = jnp.where(n % 16 == g, 1.0, 0.0).astype(BF16)
        spread_out = jnp.dot(columns * pick_group, spread, preferred_element_type=F32)
        out_ref[g] = spread_out.astype(BF16) * keep


def slots_along(axis, me):
    out = []
    for d in range(4):
        at = (me + d) % 4
        out.append({X: at * 128, Y: at * 32, Z: at % 2 * 16 + at // 2 * 4}[axis])
    return out


def chip_sums_kernel(first, width, axes, here_ref, owner_ref, weights, table, got_ref, *rest):
    outs, sums = rest[-5:-1], rest[-1]
    core = here_ref[3]
    for g in range(16):
        rows = slice(32 * g, 32 * g + 32)
        own = table[:, rows, first : first + width].reshape(128, width)
        values = jnp.concatenate([own, got_ref[:, rows, :].reshape(128, width)])
        done = jnp.dot(weights[g], values, preferred_element_type=F32)
        sums[rows] = done.astype(BF16).reshape(32, 8, width)
    along = {axis: slots_along(axis, here_ref[k]) for k, axis in enumerate((X, Y, Z))}
    parts = []
    for on_0, on_1 in zip(*axes):
        if on_0 == on_1:
            parts.append(along[on_0])
        else:
            parts.append([jnp.where(core == 0, v0, v1) for v0, v1 in zip(along[on_0], along[on_1])])
    for a in range(4):
        for b in range(4):
            for c in range(4):
                chip = parts[0][a] + parts[1][b] + parts[2][c]
                for q in range(8):
                    slot = chip + q // 4 * 8 + q % 4
                    outs[a][(b * 4 + c) * 8 + q] = sums[owner_ref[slot]]


def chip_sums(piece, here, owner_table, weights, table, got, *after):
    first, width, colour = piece
    return kernel_call(
        functools.partial(chip_sums_kernel, first, width, COLOURS[colour][2]),
        20,
        width * 1_000_000,
        out_shape=[jax.ShapeDtypeStruct((128, 8, width), BF16)] * 4,
        in_specs=[SMEM, SMEM, VMEM, VMEM, VMEM] + [HBM] * len(after),
        out_specs=[VMEM] * 4,
        scratch_shapes=[pltpu.VMEM((512, 8, width), BF16)],
    )(here, owner_table, weights, table, got, *after)


def add_kernel(pieces, *refs):
    ins, outs = refs[: 4 * pieces], refs[-4:]
    count = outs[0].shape[0]
    for d, out in enumerate(outs):
        part = pl.ds(d * count, count)
        lane = 0
        for k in range(pieces):
            own, a, b, c = ins[4 * k : 4 * k + 4]
            total = own[part].astype(F32) + a[part].astype(F32)
            total = total + b[part].astype(F32) + c[part].astype(F32)
            out[:, :, lane : lane + own.shape[2]] = total.astype(out.dtype)
            lane += own.shape[2]


def add_blocks(pieces, *after):
    count, rows, _ = pieces[0][0].shape
    width = sum(parts[0].shape[2] for parts in pieces)
    return kernel_call(
        functools.partial(add_kernel, len(pieces)),
        12,
        count * width * 64,
        out_shape=[jax.ShapeDtypeStruct((count // 4, rows, width), F32 if d == 0 else BF16) for d in range(4)],
        in_specs=[VMEM] * (4 * len(pieces)) + [HBM] * len(after),
        out_specs=[VMEM] * 4,
    )(*[block for parts in pieces for block in parts], *after)


def finish_kernel(core_ref, order_ref, *refs):
    ins, (own_ref, send_ref, cross_ref) = refs[:-3], refs[-3:]
    core = core_ref[0]
    for colour, (first, width, _) in enumerate(COLOURS):
        lane = slice(first, first + width)
        ell = lax.broadcasted_iota(jnp.int32, (8, width), 1) + core * 1024 + first
        totals = [jnp.zeros((8, width), F32) for _ in range(4)]
        parts = ins[4 * colour : 4 * colour + 4]

        def slot_sum(slot):
            h = parts[0][slot].astype(F32) + parts[1][slot].astype(F32)
            h = h + parts[2][slot].astype(F32) + parts[3][slot].astype(F32)
            order = order_ref[slot]
            h = jnp.where(ell >= order, h, 0.0)
            weighted = h * jnp.where(order == 0, 1.0, 2.0)
            for delta in range(4):
                other = pltpu.roll(h, 8 - 2 * delta, 0) if delta else h
                totals[delta] = totals[delta] + weighted * other
            return h

        for j in range(4):
            own_ref[j, :, lane] = slot_sum(core * 4 + j)
            send_ref[j, :, lane] = slot_sum((1 - core) * 4 + j)
        row = 0
        for i in range(4):
            for j in range(i, 4):
                t = totals[j - i]
                cross_ref[row : row + 1, lane] = t[2 * i : 2 * i + 1] + t[2 * i + 1 : 2 * i + 2]
                row += 1


def finish(core, orders, parts):
    return kernel_call(
        finish_kernel,
        4,
        8 * 8 * 1024 * 16,
        out_shape=[
            jax.ShapeDtypeStruct((4, 8, 1024), F32),
            jax.ShapeDtypeStruct((4, 8, 1024), F32),
            jax.ShapeDtypeStruct((10, 1024), F32),
        ],
        in_specs=[SMEM, SMEM] + [VMEM] * len(parts),
        out_specs=[VMEM] * 3,
    )(core, orders, *parts)


def steps(sky_maps, legendre, owner_table):
    my_index = lax.axis_index(BLK_GRP)
    here = places(my_index)
    core = here[CORE]
    core_scalar = core.reshape(1).astype(jnp.int32)

    here_scalars = jnp.stack([here[axis] for axis in (X, Y, Z, CORE)]).astype(jnp.int32)

    own_f, send_f, half = fourier_and_half(*PIECES[0][:2], core_scalar, legendre, sky_maps)
    got_f = swap_cores(send_f)
    received = [swap_cores(half)]
    halves = later_halves(core_scalar, legendre)
    received += [swap_cores(half) for half in halves]
    weights, table = weights_and_own_half(core_scalar, legendre, own_f, got_f, *halves)

    def exchange(sent, stage, colour):
        axes = COLOURS[colour][2]
        now = (axes[0][stage], axes[1][stage])
        return [sent[0]] + [shift_along(sent[d], now, d) for d in SHIFTS]

    pieces = [[], []]
    after = []
    for piece, got in zip(PIECES, received):
        sent = chip_sums(piece, here_scalars, owner_table, weights, table, got, *after)
        pieces[piece[2]].append(exchange(sent, 0, piece[2]))
        after = sent[:1]
    last, after = [], []
    for stage in (1, 2):
        for colour in range(2):
            sent = add_blocks(pieces[colour], *after)
            after = sent[:1]
            pieces[colour] = [exchange(sent, stage, colour)]
    last = pieces[0][0] + pieces[1][0]

    first_slot = index_of({**here, CORE: 0}) * 4
    chip_orders = jnp.concatenate(
        [lax.dynamic_slice_in_dim(owner_table, first_slot + 8 * c, 4) for c in range(2)]
    )
    own, send, cross = finish(core_scalar, chip_orders, last)
    got = swap_cores(send)

    terms = jnp.transpose(cross.reshape(10, 64, 16), (1, 0, 2)).reshape(64, 160)
    nothing = jnp.zeros_like(terms)
    terms = jnp.concatenate([jnp.where(core == 0, terms, nothing), jnp.where(core == 1, terms, nothing)])
    power = lax.all_to_all(terms, BLK_GRP, 0, 0, tiled=True)
    power = jnp.sum(power, axis=0).reshape(10, 16)
    ells = my_index * 16 + lax.iota(jnp.int32, 16)
    spectra = power / (2 * ells + 1).astype(F32)[None, :]

    low, high = jnp.where(core == 0, own, got), jnp.where(core == 0, got, own)
    harmonics = jnp.concatenate([low, high], axis=-1).reshape(4, 4, 2, 2048)
    return harmonics, spectra


def solution(mesh):
    finer = Mesh(
        mesh.devices.reshape(4, 4, 2, 2, mesh.shape["grp"]),
        BLK_GRP,
    )
    in_specs = (P(None, BLK_GRP, None), P(BLK_GRP, None, None), P())
    out_specs = (P(BLK_GRP, None, None, None), P(None, BLK_GRP))
    return jax.shard_map(steps, mesh=finer, in_specs=in_specs, out_specs=out_specs, check_vma=False)
```

profile of v0, /device:TPU:0, one launch (start us, length us, event | category | flops | bytes accessed | tf_op | source)
XLA Modules:
  0.0 116.4 jit_solution(18151810583701074885)
XLA Ops:
  0.7 3.8 %shard_map.59 = (bf16[256,128]{1,0:T(8,128)(2,1)}, bf16[256,128]{1,0:T(8,128)(2,1)}, bf16[4,512,384]{2,1,0:T(8,128)(2,1)}) custom-call(s32[1]{0:T(128)} %bitcast.core_ref, bf16[4,512,2048]{2,1,0:T(8,128)(2,1)} %leg_ref.5, f32[4,4,4096]{2,1,0:T(4,128)} %sky_ref.1, f32[320,128]{1,0:T(8,128)} %constant.117.clone.waves_ref), custom_call_target="tpu_custom_call" | custom-call | flops 3145728 | bytes 1048576 | tf_op jit(solution)/shard_map/pallas_call | solution.py:179
  4.6 3.2 %shard_map.60 = (bf16[4,512,384]{2,1,0:T(8,128)(2,1)}, bf16[4,512,256]{2,1,0:T(8,128)(2,1)}) custom-call(s32[1]{0:T(128)} %bitcast.core_ref, bf16[4,512,2048]{2,1,0:T(8,128)(2,1)} %leg_ref.5), custom_call_target="tpu_custom_call" | custom-call | flops 1048576 | bytes 1048576 | tf_op jit(solution)/shard_map/pallas_call | solution.py:82
  9.0 4.3 %collective-permute-done.got_ref = bf16[256,128]{1,0:T(8,128)(2,1)S(1)} collective-permute-done((bf16[256,128]{1,0:T(8,128)(2,1)S(1)}, bf16[256,128]{1,0:T(8,128)(2,1)S(1)}, u32[]{:S(2)}, u32[]{:S(2)}) %collective-permute-start) | collective-permute-done | bytes 65568 | tf_op jit(solution)/shard_map/ppermute | solution.py:52
  13.3 2.8 %shard_map.61 = (bf16[16,256,256]{2,1,0:T(8,128)(2,1)S(1)}, bf16[4,512,1024]{2,1,0:T(8,128)(2,1)S(1)}) custom-call(s32[1]{0:T(128)} %bitcast.core_ref, bf16[4,512,2048]{2,1,0:T(8,128)(2,1)} %leg_ref.5, bf16[256,128]{1,0:T(8,128)(2,1)S(1)} %copy-done, bf16[256,128]{1,0:T(8,128)(2,1)S(1)} %collective-permute-done.got_ref, ...), custom_call_target="tpu_custom_call" | custom-call | flops 67108864 | bytes 1048576 | tf_op jit(solution)/shard_map/pallas_call | solution.py:207
  16.1 2.4 %shard_map.62 = (bf16[128,8,384]{2,1,0:T(8,128)(2,1)S(1)}, bf16[128,8,384]{2,1,0:T(8,128)(2,1)S(1)}, bf16[128,8,384]{2,1,0:T(8,128)(2,1)S(1)}, bf16[128,8,384]{2,1,0:T(8,128)(2,1)S(1)}) custom-call(s32[4]{0:T(128)S(1)} %pad_add_fusion.1.here_ref, s32[512]{0:T(512)S(1)} %copy-done.1, bf16[16,256,256]{2,1,0:T(8,128)(2,1)S(1)} %get-tuple-element.44.weights, ...), custom_call_target="tpu_custom_call" | custom-call | flops 384000000 | bytes 1048576 | tf_op jit(solution)/shard_map/pallas_call | solution.py:266
  18.5 3.2 %collective-permute-start.2 = (bf16[128,8,384]{2,1,0:T(8,128)(2,1)S(1)}, bf16[128,8,384]{2,1,0:T(8,128)(2,1)S(1)}, u32[]{:S(2)}, u32[]{:S(2)}) collective-permute-start(bf16[128,8,384]{2,1,0:T(8,128)(2,1)S(1)} %get-tuple-element.48), channel_id=1, source_target_pairs={{0,64},{1,65},{2,18},{3,19},{4,68},{5,69},{6,22},{7,23},{8,72},{9,... | collective-permute-start | bytes 2359304 | tf_op jit(solution)/shard_map/ppermute | solution.py:48
  22.3 2.6 %collective-permute-start.4 = (bf16[128,8,384]{2,1,0:T(8,128)(2,1)S(1)}, bf16[128,8,384]{2,1,0:T(8,128)(2,1)S(1)}, u32[]{:S(2)}, u32[]{:S(2)}) collective-permute-start(bf16[128,8,384]{2,1,0:T(8,128)(2,1)S(1)} %get-tuple-element.50), channel_id=1, source_target_pairs={{0,96},{1,97},{2,26},{3,27},{4,100},{5,101},{6,30},{7,31},{8,104},... | collective-permute-start | bytes 2359304 | tf_op jit(solution)/shard_map/ppermute | solution.py:48
  25.0 2.4 %shard_map.63 = (bf16[128,8,384]{2,1,0:T(8,128)(2,1)S(1)}, bf16[128,8,384]{2,1,0:T(8,128)(2,1)S(1)}, bf16[128,8,384]{2,1,0:T(8,128)(2,1)S(1)}, bf16[128,8,384]{2,1,0:T(8,128)(2,1)S(1)}) custom-call(s32[4]{0:T(128)S(1)} %pad_add_fusion.1.here_ref, s32[512]{0:T(512)S(1)} %copy-done.1, bf16[16,256,256]{2,1,0:T(8,128)(2,1)S(1)} %get-tuple-element.44.weights, ...), custom_call_target="tpu_custom_call" | custom-call | flops 384000000 | bytes 1048576 | tf_op jit(solution)/shard_map/pallas_call | solution.py:266
  28.3 3.8 %collective-permute-done.2.refs_1_ = bf16[128,8,384]{2,1,0:T(8,128)(2,1)S(1)} collective-permute-done((bf16[128,8,384]{2,1,0:T(8,128)(2,1)S(1)}, bf16[128,8,384]{2,1,0:T(8,128)(2,1)S(1)}, u32[]{:S(2)}, u32[]{:S(2)}) %collective-permute-start.2) | collective-permute-done | bytes 786464 | tf_op jit(solution)/shard_map/ppermute | solution.py:48
  32.2 2.9 %collective-permute-start.8 = (bf16[128,8,384]{2,1,0:T(8,128)(2,1)S(1)}, bf16[128,8,384]{2,1,0:T(8,128)(2,1)S(1)}, u32[]{:S(2)}, u32[]{:S(2)}) collective-permute-start(bf16[128,8,384]{2,1,0:T(8,128)(2,1)S(1)} %get-tuple-element.54), channel_id=1, source_target_pairs={{0,96},{1,97},{2,26},{3,27},{4,100},{5,101},{6,30},{7,31},{8,104},... | collective-permute-start | bytes 2359304 | tf_op jit(solution)/shard_map/ppermute | solution.py:48
  35.1 2.5 %shard_map.65 = (bf16[128,8,256]{2,1,0:T(8,128)(2,1)S(1)}, bf16[128,8,256]{2,1,0:T(8,128)(2,1)S(1)}, bf16[128,8,256]{2,1,0:T(8,128)(2,1)S(1)}, bf16[128,8,256]{2,1,0:T(8,128)(2,1)S(1)}) custom-call(s32[4]{0:T(128)S(1)} %pad_add_fusion.1.here_ref, s32[512]{0:T(512)S(1)} %copy-done.1, bf16[16,256,256]{2,1,0:T(8,128)(2,1)S(1)} %get-tuple-element.44.weights, ...), custom_call_target="tpu_custom_call" | custom-call | flops 256000000 | bytes 1048576 | tf_op jit(solution)/shard_map/pallas_call | solution.py:266
  37.6 2.9 %collective-permute-done.3.refs_2_ = bf16[128,8,384]{2,1,0:T(8,128)(2,1)S(1)} collective-permute-done((bf16[128,8,384]{2,1,0:T(8,128)(2,1)S(1)}, bf16[128,8,384]{2,1,0:T(8,128)(2,1)S(1)}, u32[]{:S(2)}, u32[]{:S(2)}) %collective-permute-start.3) | collective-permute-done | bytes 786464 | tf_op jit(solution)/shard_map/ppermute | solution.py:48
  40.5 4.0 %collective-permute-start.13 = (bf16[128,8,256]{2,1,0:T(8,128)(2,1)S(1)}, bf16[128,8,256]{2,1,0:T(8,128)(2,1)S(1)}, u32[]{:S(2)}, u32[]{:S(2)}) collective-permute-start(bf16[128,8,256]{2,1,0:T(8,128)(2,1)S(1)} %get-tuple-element.60), channel_id=1, source_target_pairs={{0,1},{1,0},{2,3},{3,2},{4,5},{5,4},{6,7},{7,6},{8,9},{9,8},{10,11... | collective-permute-start | bytes 1572872 | tf_op jit(solution)/shard_map/ppermute | solution.py:48
  45.5 3.6 %collective-permute-done.6.refs_5_ = bf16[128,8,384]{2,1,0:T(8,128)(2,1)S(1)} collective-permute-done((bf16[128,8,384]{2,1,0:T(8,128)(2,1)S(1)}, bf16[128,8,384]{2,1,0:T(8,128)(2,1)S(1)}, u32[]{:S(2)}, u32[]{:S(2)}) %collective-permute-start.6) | collective-permute-done | bytes 786464 | tf_op jit(solution)/shard_map/ppermute | solution.py:48
  49.1 4.1 %collective-permute-start.15 = (bf16[128,8,256]{2,1,0:T(8,128)(2,1)S(1)}, bf16[128,8,256]{2,1,0:T(8,128)(2,1)S(1)}, u32[]{:S(2)}, u32[]{:S(2)}) collective-permute-start(bf16[128,8,256]{2,1,0:T(8,128)(2,1)S(1)} %get-tuple-element.62), channel_id=1, source_target_pairs={{0,5},{1,4},{2,7},{3,6},{4,0},{5,1},{6,2},{7,3},{8,13},{9,12},{10,... | collective-permute-start | bytes 1572872 | tf_op jit(solution)/shard_map/ppermute | solution.py:48
  53.2 4.1 %collective-permute-done.7.refs_6_ = bf16[128,8,384]{2,1,0:T(8,128)(2,1)S(1)} collective-permute-done((bf16[128,8,384]{2,1,0:T(8,128)(2,1)S(1)}, bf16[128,8,384]{2,1,0:T(8,128)(2,1)S(1)}, u32[]{:S(2)}, u32[]{:S(2)}) %collective-permute-start.7) | collective-permute-done | bytes 786464 | tf_op jit(solution)/shard_map/ppermute | solution.py:48
  59.0 3.2 %collective-permute-start.9 = (bf16[32,8,768]{2,1,0:T(8,128)(2,1)S(1)}, bf16[32,8,768]{2,1,0:T(8,128)(2,1)S(1)}, u32[]{:S(2)}, u32[]{:S(2)}) collective-permute-start(bf16[32,8,768]{2,1,0:T(8,128)(2,1)S(1)} %get-tuple-element.56), channel_id=1, source_target_pairs={{0,16},{1,17},{2,3},{3,2},{4,20},{5,21},{6,7},{7,6},{8,24},{9,25},... | collective-permute-start | bytes 1179656 | tf_op jit(solution)/shard_map/ppermute | solution.py:48
  62.9 2.6 %collective-permute-start.11 = (bf16[32,8,768]{2,1,0:T(8,128)(2,1)S(1)}, bf16[32,8,768]{2,1,0:T(8,128)(2,1)S(1)}, u32[]{:S(2)}, u32[]{:S(2)}) collective-permute-start(bf16[32,8,768]{2,1,0:T(8,128)(2,1)S(1)} %get-tuple-element.58), channel_id=1, source_target_pairs={{0,24},{1,25},{2,7},{3,6},{4,28},{5,29},{6,2},{7,3},{8,0},{9,1},{1... | collective-permute-start | bytes 1179656 | tf_op jit(solution)/shard_map/ppermute | solution.py:48
  65.4 3.2 %collective-permute-done.14.refs_2_ = bf16[128,8,256]{2,1,0:T(8,128)(2,1)S(1)} collective-permute-done((bf16[128,8,256]{2,1,0:T(8,128)(2,1)S(1)}, bf16[128,8,256]{2,1,0:T(8,128)(2,1)S(1)}, u32[]{:S(2)}, u32[]{:S(2)}) %collective-permute-start.14) | collective-permute-done | bytes 524320 | tf_op jit(solution)/shard_map/ppermute | solution.py:48
  72.5 3.2 %collective-permute-start.21 = (bf16[32,8,256]{2,1,0:T(8,128)(2,1)S(1)}, bf16[32,8,256]{2,1,0:T(8,128)(2,1)S(1)}, u32[]{:S(2)}, u32[]{:S(2)}) collective-permute-start(bf16[32,8,256]{2,1,0:T(8,128)(2,1)S(1)} %get-tuple-element.70), channel_id=1, source_target_pairs={{0,96},{1,97},{2,98},{3,99},{4,100},{5,101},{6,102},{7,103},{8,104... | collective-permute-start | bytes 393224 | tf_op jit(solution)/shard_map/ppermute | solution.py:48
  79.3 4.0 %collective-permute-start.22 = (bf16[8,8,256]{2,1,0:T(8,128)(2,1)S(1)}, bf16[8,8,256]{2,1,0:T(8,128)(2,1)S(1)}, u32[]{:S(2)}, u32[]{:S(2)}) collective-permute-start(bf16[8,8,256]{2,1,0:T(8,128)(2,1)S(1)} %get-tuple-element.72), channel_id=1, source_target_pairs={{0,16},{1,17},{2,18},{3,19},{4,20},{5,21},{6,22},{7,23},{8,24},{9,... | collective-permute-start | bytes 98312 | tf_op jit(solution)/shard_map/ppermute | solution.py:48
  84.6 4.1 %collective-permute-start.17 = (bf16[8,8,768]{2,1,0:T(8,128)(2,1)S(1)}, bf16[8,8,768]{2,1,0:T(8,128)(2,1)S(1)}, u32[]{:S(2)}, u32[]{:S(2)}) collective-permute-start(bf16[8,8,768]{2,1,0:T(8,128)(2,1)S(1)} %get-tuple-element.66), channel_id=1, source_target_pairs={{0,4},{1,5},{2,34},{3,35},{4,1},{5,0},{6,38},{7,39},{8,12},{9,13},... | collective-permute-start | bytes 294920 | tf_op jit(solution)/shard_map/ppermute | solution.py:48
  96.1 9.3 %all-to-all-start = ((f32[128,1,160]{2,1,0:T(1,128)}), f32[128,1,160]{2,1,0:T(1,128)S(1)}, u32[]{:S(2)}, u32[]{:S(2)}) async-start(f32[128,1,160]{2,1,0:T(1,128)} %copy.10), calls=%async_computation | async-start | bytes 262144 | tf_op jit(solution)/shard_map/all_to_all | solution.py:394
  105.6 9.1 %all-to-all-done = f32[128,1,160]{2,1,0:T(1,128)S(1)} async-done(((f32[128,1,160]{2,1,0:T(1,128)}), f32[128,1,160]{2,1,0:T(1,128)S(1)}, u32[]{:S(2)}, u32[]{:S(2)}) %all-to-all-start) | async-done | bytes 81952 | tf_op jit(solution)/shard_map/all_to_all | solution.py:394
  (64 shorter events, 24.0 us)
Async XLA Ops:
  4.5 11.6 %collective-permute-start.1 = (bf16[4,512,384]{2,1,0:T(8,128)(2,1)}, bf16[4,512,384]{2,1,0:T(8,128)(2,1)S(1)}, u32[]{:S(2)}, u32[]{:S(2)}) collective-permute-start(bf16[4,512,384]{2,1,0:T(8,128)(2,1)} %get-tuple-element.46), channel_id=1, source_target_pairs={{0,2},{2,0},{1,3},{3,1},{4,6},{6,4},{5,7},{7,5},{8,10},{10,8},{9,1... | collective-permute-start | bytes 4718600 | tf_op jit(solution)/shard_map/ppermute | solution.py:52
  7.8 17.2 %collective-permute-start.5 = (bf16[4,512,384]{2,1,0:T(8,128)(2,1)}, bf16[4,512,384]{2,1,0:T(8,128)(2,1)S(1)}, u32[]{:S(2)}, u32[]{:S(2)}) collective-permute-start(bf16[4,512,384]{2,1,0:T(8,128)(2,1)} %get-tuple-element.42.rest_0_), channel_id=1, source_target_pairs={{0,2},{2,0},{1,3},{3,1},{4,6},{6,4},{5,7},{7,5},{8,10},{10,8},{9,1... | collective-permute-start | bytes 4718600 | tf_op jit(solution)/shard_map/ppermute | solution.py:52
  8.4 19.1 %collective-permute-start.12 = (bf16[4,512,256]{2,1,0:T(8,128)(2,1)}, bf16[4,512,256]{2,1,0:T(8,128)(2,1)}, u32[]{:S(2)}, u32[]{:S(2)}) collective-permute-start(bf16[4,512,256]{2,1,0:T(8,128)(2,1)} %get-tuple-element.43.rest_1_), channel_id=1, source_target_pairs={{0,2},{2,0},{1,3},{3,1},{4,6},{6,4},{5,7},{7,5},{8,10},{10,8},{9,1... | collective-permute-start | bytes 3145736 | tf_op jit(solution)/shard_map/ppermute | solution.py:52
  18.5 13.7 %collective-permute-start.2 = (bf16[128,8,384]{2,1,0:T(8,128)(2,1)S(1)}, bf16[128,8,384]{2,1,0:T(8,128)(2,1)S(1)}, u32[]{:S(2)}, u32[]{:S(2)}) collective-permute-start(bf16[128,8,384]{2,1,0:T(8,128)(2,1)S(1)} %get-tuple-element.48), channel_id=1, source_target_pairs={{0,64},{1,65},{2,18},{3,19},{4,68},{5,69},{6,22},{7,23},{8,72},{9,... | collective-permute-start | bytes 2359304 | tf_op jit(solution)/shard_map/ppermute | solution.py:48
  21.7 18.8 %collective-permute-start.3 = (bf16[128,8,384]{2,1,0:T(8,128)(2,1)S(1)}, bf16[128,8,384]{2,1,0:T(8,128)(2,1)S(1)}, u32[]{:S(2)}, u32[]{:S(2)}) collective-permute-start(bf16[128,8,384]{2,1,0:T(8,128)(2,1)S(1)} %get-tuple-element.49), channel_id=1, source_target_pairs={{0,32},{1,33},{2,10},{3,11},{4,36},{5,37},{6,14},{7,15},{8,40},{9,... | collective-permute-start | bytes 2359304 | tf_op jit(solution)/shard_map/ppermute | solution.py:48
  22.3 22.2 %collective-permute-start.4 = (bf16[128,8,384]{2,1,0:T(8,128)(2,1)S(1)}, bf16[128,8,384]{2,1,0:T(8,128)(2,1)S(1)}, u32[]{:S(2)}, u32[]{:S(2)}) collective-permute-start(bf16[128,8,384]{2,1,0:T(8,128)(2,1)S(1)} %get-tuple-element.50), channel_id=1, source_target_pairs={{0,96},{1,97},{2,26},{3,27},{4,100},{5,101},{6,30},{7,31},{8,104},... | collective-permute-start | bytes 2359304 | tf_op jit(solution)/shard_map/ppermute | solution.py:48
  27.4 21.7 %collective-permute-start.6 = (bf16[128,8,384]{2,1,0:T(8,128)(2,1)S(1)}, bf16[128,8,384]{2,1,0:T(8,128)(2,1)S(1)}, u32[]{:S(2)}, u32[]{:S(2)}) collective-permute-start(bf16[128,8,384]{2,1,0:T(8,128)(2,1)S(1)} %get-tuple-element.52), channel_id=1, source_target_pairs={{0,64},{1,65},{2,18},{3,19},{4,68},{5,69},{6,22},{7,23},{8,72},{9,... | collective-permute-start | bytes 2359304 | tf_op jit(solution)/shard_map/ppermute | solution.py:48
  27.5 29.9 %collective-permute-start.7 = (bf16[128,8,384]{2,1,0:T(8,128)(2,1)S(1)}, bf16[128,8,384]{2,1,0:T(8,128)(2,1)S(1)}, u32[]{:S(2)}, u32[]{:S(2)}) collective-permute-start(bf16[128,8,384]{2,1,0:T(8,128)(2,1)S(1)} %get-tuple-element.53), channel_id=1, source_target_pairs={{0,32},{1,33},{2,10},{3,11},{4,36},{5,37},{6,14},{7,15},{8,40},{9,... | collective-permute-start | bytes 2359304 | tf_op jit(solution)/shard_map/ppermute | solution.py:48
  32.2 25.5 %collective-permute-start.8 = (bf16[128,8,384]{2,1,0:T(8,128)(2,1)S(1)}, bf16[128,8,384]{2,1,0:T(8,128)(2,1)S(1)}, u32[]{:S(2)}, u32[]{:S(2)}) collective-permute-start(bf16[128,8,384]{2,1,0:T(8,128)(2,1)S(1)} %get-tuple-element.54), channel_id=1, source_target_pairs={{0,96},{1,97},{2,26},{3,27},{4,100},{5,101},{6,30},{7,31},{8,104},... | collective-permute-start | bytes 2359304 | tf_op jit(solution)/shard_map/ppermute | solution.py:48
  40.5 22.3 %collective-permute-start.13 = (bf16[128,8,256]{2,1,0:T(8,128)(2,1)S(1)}, bf16[128,8,256]{2,1,0:T(8,128)(2,1)S(1)}, u32[]{:S(2)}, u32[]{:S(2)}) collective-permute-start(bf16[128,8,256]{2,1,0:T(8,128)(2,1)S(1)} %get-tuple-element.60), channel_id=1, source_target_pairs={{0,1},{1,0},{2,3},{3,2},{4,5},{5,4},{6,7},{7,6},{8,9},{9,8},{10,11... | collective-permute-start | bytes 1572872 | tf_op jit(solution)/shard_map/ppermute | solution.py:48
  44.5 24.1 %collective-permute-start.14 = (bf16[128,8,256]{2,1,0:T(8,128)(2,1)S(1)}, bf16[128,8,256]{2,1,0:T(8,128)(2,1)S(1)}, u32[]{:S(2)}, u32[]{:S(2)}) collective-permute-start(bf16[128,8,256]{2,1,0:T(8,128)(2,1)S(1)} %get-tuple-element.61), channel_id=1, source_target_pairs={{0,4},{1,5},{2,6},{3,7},{4,1},{5,0},{6,3},{7,2},{8,12},{9,13},{10,... | collective-permute-start | bytes 1572872 | tf_op jit(solution)/shard_map/ppermute | solution.py:48
  49.1 20.4 %collective-permute-start.15 = (bf16[128,8,256]{2,1,0:T(8,128)(2,1)S(1)}, bf16[128,8,256]{2,1,0:T(8,128)(2,1)S(1)}, u32[]{:S(2)}, u32[]{:S(2)}) collective-permute-start(bf16[128,8,256]{2,1,0:T(8,128)(2,1)S(1)} %get-tuple-element.62), channel_id=1, source_target_pairs={{0,5},{1,4},{2,7},{3,6},{4,0},{5,1},{6,2},{7,3},{8,13},{9,12},{10,... | collective-permute-start | bytes 1572872 | tf_op jit(solution)/shard_map/ppermute | solution.py:48
  59.0 13.5 %collective-permute-start.9 = (bf16[32,8,768]{2,1,0:T(8,128)(2,1)S(1)}, bf16[32,8,768]{2,1,0:T(8,128)(2,1)S(1)}, u32[]{:S(2)}, u32[]{:S(2)}) collective-permute-start(bf16[32,8,768]{2,1,0:T(8,128)(2,1)S(1)} %get-tuple-element.56), channel_id=1, source_target_pairs={{0,16},{1,17},{2,3},{3,2},{4,20},{5,21},{6,7},{7,6},{8,24},{9,25},... | collective-permute-start | bytes 1179656 | tf_op jit(solution)/shard_map/ppermute | solution.py:48
  62.2 13.6 %collective-permute-start.10 = (bf16[32,8,768]{2,1,0:T(8,128)(2,1)}, bf16[32,8,768]{2,1,0:T(8,128)(2,1)S(1)}, u32[]{:S(2)}, u32[]{:S(2)}) collective-permute-start(bf16[32,8,768]{2,1,0:T(8,128)(2,1)} %get-tuple-element.57), channel_id=1, source_target_pairs={{0,8},{1,9},{2,6},{3,7},{4,12},{5,13},{6,3},{7,2},{8,16},{9,17},{1... | collective-permute-start | bytes 1179656 | tf_op jit(solution)/shard_map/ppermute | solution.py:48
  62.9 12.9 %collective-permute-start.11 = (bf16[32,8,768]{2,1,0:T(8,128)(2,1)S(1)}, bf16[32,8,768]{2,1,0:T(8,128)(2,1)S(1)}, u32[]{:S(2)}, u32[]{:S(2)}) collective-permute-start(bf16[32,8,768]{2,1,0:T(8,128)(2,1)S(1)} %get-tuple-element.58), channel_id=1, source_target_pairs={{0,24},{1,25},{2,7},{3,6},{4,28},{5,29},{6,2},{7,3},{8,0},{9,1},{1... | collective-permute-start | bytes 1179656 | tf_op jit(solution)/shard_map/ppermute | solution.py:48
  70.3 7.7 %collective-permute-start.19 = (bf16[32,8,256]{2,1,0:T(8,128)(2,1)}, bf16[32,8,256]{2,1,0:T(8,128)(2,1)S(1)}, u32[]{:S(2)}, u32[]{:S(2)}) collective-permute-start(bf16[32,8,256]{2,1,0:T(8,128)(2,1)} %get-tuple-element.68), channel_id=1, source_target_pairs={{0,64},{1,65},{2,66},{3,67},{4,68},{5,69},{6,70},{7,71},{8,72},{9,... | collective-permute-start | bytes 393224 | tf_op jit(solution)/shard_map/ppermute | solution.py:48
  72.5 6.7 %collective-permute-start.20 = (bf16[32,8,256]{2,1,0:T(8,128)(2,1)S(1)}, bf16[32,8,256]{2,1,0:T(8,128)(2,1)S(1)}, u32[]{:S(2)}, u32[]{:S(2)}) collective-permute-start(bf16[32,8,256]{2,1,0:T(8,128)(2,1)S(1)} %get-tuple-element.69), channel_id=1, source_target_pairs={{0,32},{1,33},{2,34},{3,35},{4,36},{5,37},{6,38},{7,39},{8,40},{9,... | collective-permute-start | bytes 393224 | tf_op jit(solution)/shard_map/ppermute | solution.py:48
  72.5 6.7 %collective-permute-start.21 = (bf16[32,8,256]{2,1,0:T(8,128)(2,1)S(1)}, bf16[32,8,256]{2,1,0:T(8,128)(2,1)S(1)}, u32[]{:S(2)}, u32[]{:S(2)}) collective-permute-start(bf16[32,8,256]{2,1,0:T(8,128)(2,1)S(1)} %get-tuple-element.70), channel_id=1, source_target_pairs={{0,96},{1,97},{2,98},{3,99},{4,100},{5,101},{6,102},{7,103},{8,104... | collective-permute-start | bytes 393224 | tf_op jit(solution)/shard_map/ppermute | solution.py:48
  79.3 10.3 %collective-permute-start.22 = (bf16[8,8,256]{2,1,0:T(8,128)(2,1)S(1)}, bf16[8,8,256]{2,1,0:T(8,128)(2,1)S(1)}, u32[]{:S(2)}, u32[]{:S(2)}) collective-permute-start(bf16[8,8,256]{2,1,0:T(8,128)(2,1)S(1)} %get-tuple-element.72), channel_id=1, source_target_pairs={{0,16},{1,17},{2,18},{3,19},{4,20},{5,21},{6,22},{7,23},{8,24},{9,... | collective-permute-start | bytes 98312 | tf_op jit(solution)/shard_map/ppermute | solution.py:48
  83.4 10.5 %collective-permute-start.16 = (bf16[8,8,768]{2,1,0:T(8,128)(2,1)S(1)}, bf16[8,8,768]{2,1,0:T(8,128)(2,1)S(1)}, u32[]{:S(2)}, u32[]{:S(2)}) collective-permute-start(bf16[8,8,768]{2,1,0:T(8,128)(2,1)S(1)} %get-tuple-element.65), channel_id=1, source_target_pairs={{0,1},{1,0},{2,66},{3,67},{4,5},{5,4},{6,70},{7,71},{8,9},{9,8},{1... | collective-permute-start | bytes 294920 | tf_op jit(solution)/shard_map/ppermute | solution.py:48
  84.6 9.3 %collective-permute-start.17 = (bf16[8,8,768]{2,1,0:T(8,128)(2,1)S(1)}, bf16[8,8,768]{2,1,0:T(8,128)(2,1)S(1)}, u32[]{:S(2)}, u32[]{:S(2)}) collective-permute-start(bf16[8,8,768]{2,1,0:T(8,128)(2,1)S(1)} %get-tuple-element.66), channel_id=1, source_target_pairs={{0,4},{1,5},{2,34},{3,35},{4,1},{5,0},{6,38},{7,39},{8,12},{9,13},... | collective-permute-start | bytes 294920 | tf_op jit(solution)/shard_map/ppermute | solution.py:48
  88.8 5.1 %collective-permute-start.18 = (bf16[8,8,768]{2,1,0:T(8,128)(2,1)S(1)}, bf16[8,8,768]{2,1,0:T(8,128)(2,1)S(1)}, u32[]{:S(2)}, u32[]{:S(2)}) collective-permute-start(bf16[8,8,768]{2,1,0:T(8,128)(2,1)S(1)} %get-tuple-element.67), channel_id=1, source_target_pairs={{0,5},{1,4},{2,98},{3,99},{4,0},{5,1},{6,102},{7,103},{8,13},{9,12... | collective-permute-start | bytes 294920 | tf_op jit(solution)/shard_map/ppermute | solution.py:48
  96.1 18.6 %all-to-all-start = ((f32[128,1,160]{2,1,0:T(1,128)}), f32[128,1,160]{2,1,0:T(1,128)S(1)}, u32[]{:S(2)}, u32[]{:S(2)}) async-start(f32[128,1,160]{2,1,0:T(1,128)} %copy.10), calls=%async_computation | async-start | bytes 262144 | tf_op jit(solution)/shard_map/all_to_all | solution.py:394
  105.5 10.1 %collective-permute-start.25 = (f32[4,8,1024]{2,1,0:T(8,128)S(1)}, f32[4,8,1024]{2,1,0:T(8,128)S(1)}, u32[]{:S(2)}, u32[]{:S(2)}) collective-permute-start(f32[4,8,1024]{2,1,0:T(8,128)S(1)} %get-tuple-element.76), channel_id=1, source_target_pairs={{0,2},{2,0},{1,3},{3,1},{4,6},{6,4},{5,7},{7,5},{8,10},{10,8},{9,1... | collective-permute-start | bytes 393224 | tf_op jit(solution)/shard_map/ppermute | solution.py:52
  (6 other events, 29.8 us)
where the time goes:
time: 118 us; the launch traced here: 116 us
  starting transfers between devices  54.5 us (46%)
  waiting for transfers between devices  37.5 us (32%)
  Pallas kernels  20.2 us (17%)
  local copies, waits for them, and re-layouts  2.32 us (2%)
    ppermute x21, starting transfers between devices, shift_along(): return lax.ppermute(x, BLK_GRP, pairs)  43.9 us
    ppermute x21, waiting for transfers between devices, shift_along(): return lax.ppermute(x, BLK_GRP, pairs)  24 us
    all_to_all x1, starting transfers between devices, steps(): power = lax.all_to_all(terms, BLK_GRP, 0, 0, tiled=True)  9.34 us
    all_to_all x1, waiting for transfers between devices, steps(): power = lax.all_to_all(terms, BLK_GRP, 0, 0, tiled=True)  9.12 us
    pallas_call x3, Pallas kernels, chip_sums(): kernel_call(functools.partial(chip_sums_kernel, first, width, COLOURS[col...  7.34 us
    ppermute x5, waiting for transfers between devices, swap_cores(): return lax.ppermute(x, CORE, [(0, 1), (1, 0)])  4.3 us
    pallas_call x1, Pallas kernels, fourier_and_half(): kernel_call(functools.partial(fourier_kernel, first, width), 55, width *...  3.79 us
    pallas_call x1, Pallas kernels, later_halves(): kernel_call(halves_kernel, 48, 1 << 20, out_shape=[jax.ShapeDtypeStruct((...  3.22 us
  transfers between devices with their start and end apart: 27, of which 12 were waited for; matrix products, arithmetic and copies ran while one was open for 1% of the time, Pallas kernels for 13%

commit v1 on v0

--- a/solution.py
+++ b/solution.py
@@ -17,7 +17,7 @@
     (0, 768, ((X, Y, Z), (Y, Z, X))),
     (768, 256, ((Z, X, Y), (Z, X, Y))),
 )
-PIECES = ((0, 384, 0), (384, 384, 0), (768, 256, 1))
+PIECES = ((0, 512, 0), (512, 256, 0), (768, 256, 1))
 SHIFTS = (2, 1, 3)
 F32, BF16 = jnp.float32, jnp.bfloat16
 SMEM = pl.BlockSpec(memory_space=pltpu.SMEM)
@@ -274,31 +274,53 @@
     )(here, owner_table, weights, table, got, *after)
 
 
-def add_kernel(pieces, *refs):
-    ins, outs = refs[: 4 * pieces], refs[-4:]
+def total_of(refs, part):
+    total = refs[0][part].astype(F32)
+    for ref in refs[1:]:
+        total = total + ref[part].astype(F32)
+    return total
+
+
+def add_kernel(counts, *refs):
+    outs = refs[-4:]
     count = outs[0].shape[0]
     for d, out in enumerate(outs):
         part = pl.ds(d * count, count)
-        lane = 0
-        for k in range(pieces):
-            own, a, b, c = ins[4 * k : 4 * k + 4]
-            total = own[part].astype(F32) + a[part].astype(F32)
-            total = total + b[part].astype(F32) + c[part].astype(F32)
-            out[:, :, lane : lane + own.shape[2]] = total.astype(out.dtype)
-            lane += own.shape[2]
+        lane, k = 0, 0
+        for n in counts:
+            total = total_of(refs[k : k + n], part)
+            out[:, :, lane : lane + total.shape[2]] = total.astype(out.dtype)
+            lane, k = lane + total.shape[2], k + n
 
 
 def add_blocks(pieces, *after):
     count, rows, _ = pieces[0][0].shape
     width = sum(parts[0].shape[2] for parts in pieces)
-    return kernel_call(
-        functools.partial(add_kernel, len(pieces)),
+    counts = [len(parts) for parts in pieces]
+    return kernel_call(
+        functools.partial(add_kernel, counts),
         12,
         count * width * 64,
         out_shape=[jax.ShapeDtypeStruct((count // 4, rows, width), F32 if d == 0 else BF16) for d in range(4)],
-        in_specs=[VMEM] * (4 * len(pieces)) + [HBM] * len(after),
+        in_specs=[VMEM] * sum(counts) + [HBM] * len(after),
         out_specs=[VMEM] * 4,
     )(*[block for parts in pieces for block in parts], *after)
+
+
+def combine_kernel(a_ref, b_ref, *rest):
+    everything = pl.ds(0, a_ref.shape[0])
+    rest[-1][...] = total_of((a_ref, b_ref), everything).astype(BF16)
+
+
+def combine(a, b, *after):
+    return kernel_call(
+        combine_kernel,
+        8,
+        a.size,
+        out_shape=jax.ShapeDtypeStruct(a.shape, BF16),
+        in_specs=[VMEM] * 2 + [HBM] * len(after),
+        out_specs=VMEM,
+    )(a, b, *after)
 
 
 def finish_kernel(core_ref, order_ref, *refs):
@@ -357,25 +379,36 @@
 
     own_f, send_f, half = fourier_and_half(*PIECES[0][:2], core_scalar, legendre, sky_maps)
     got_f = swap_cores(send_f)
-    received = [swap_cores(half)]
-    halves = later_halves(core_scalar, legendre)
-    received += [swap_cores(half) for half in halves]
-    weights, table = weights_and_own_half(core_scalar, legendre, own_f, got_f, *halves)
+    got_0 = swap_cores(half)
+    half_1, half_2 = later_halves(core_scalar, legendre)
+    got_1, got_2 = swap_cores(half_1), swap_cores(half_2)
+    weights, table = weights_and_own_half(core_scalar, legendre, own_f, got_f, half_1, half_2)
+
+    def move(block, stage, colour, shift):
+        axes = COLOURS[colour][2]
+        return shift_along(block, (axes[0][stage], axes[1][stage]), shift)
 
     def exchange(sent, stage, colour):
-        axes = COLOURS[colour][2]
-        now = (axes[0][stage], axes[1][stage])
-        return [sent[0]] + [shift_along(sent[d], now, d) for d in SHIFTS]
-
-    pieces = [[], []]
+        return [sent[0]] + [move(sent[d], stage, colour, d) for d in SHIFTS]
+
+    def sums_of(k, got, *after):
+        return chip_sums(PIECES[k], here_scalars, owner_table, weights, table, got, *after)
+
+    up = sums_of(0, got_0)
+    through_up, from_above = move(up[2], 0, 0, 1), move(up[3], 0, 0, 3)
+    down = sums_of(1, got_1)
+    through_down, from_below = move(down[2], 0, 0, 3), move(down[1], 0, 0, 1)
+    sent = sums_of(2, got_2, down[0])
+    colour_1 = [exchange(sent, 0, 1)]
+    both_up = combine(up[1], through_up, sent[0])
+    from_below_up = move(both_up, 0, 0, 1)
+    both_down = combine(down[3], through_down, both_up)
+    from_above_down = move(both_down, 0, 0, 3)
+    colour_0 = [[up[0], from_above, from_below_up], [down[0], from_below, from_above_down]]
+    pieces = [colour_0, colour_1]
     after = []
-    for piece, got in zip(PIECES, received):
-        sent = chip_sums(piece, here_scalars, owner_table, weights, table, got, *after)
-        pieces[piece[2]].append(exchange(sent, 0, piece[2]))
-        after = sent[:1]
-    last, after = [], []
     for stage in (1, 2):
-        for colour in range(2):
+        for colour in (0, 1):
             sent = add_blocks(pieces[colour], *after)
             after = sent[:1]
             pieces[colour] = [exchange(sent, stage, colour)]
@@ -397,7 +430,8 @@
     spectra = power / (2 * ells + 1).astype(F32)[None, :]
 
     low, high = jnp.where(core == 0, own, got), jnp.where(core == 0, got, own)
-    harmonics = jnp.concatenate([low, high], axis=-1).reshape(4, 4, 2, 2048)
+    harmonics = jnp.concatenate([low, high], axis=-1)
+    harmonics = harmonics.reshape(4, 4, 2, 2048)
     return harmonics, spectra
 
 

time: 118 us -> 119 us (level)
  waiting for transfers between devices: 37.5 us -> 45.1 us
  starting transfers between devices: 54.5 us -> 49.2 us
    ppermute x21, waiting for transfers between devices: 24 us -> 35.6 us  [shift_along(): return lax.ppermute(x, BLK_GRP, pairs)]
    ppermute x5, waiting for transfers between devices: 4.3 us -> 0.39 us  [swap_cores(): return lax.ppermute(x, CORE, [(0, 1), (1, 0)])]
    ppermute x21, starting transfers between devices: 43.9 us -> 40.4 us  [shift_along(): return lax.ppermute(x, BLK_GRP, pairs)]
    all_to_all x1, starting transfers between devices: 9.34 us -> 7.54 us  [steps(): power = lax.all_to_all(terms, BLK_GRP, 0, 0, tiled=True)]
  transfers between devices with their start and end apart: 27 -> 27, of which waited for: 12 -> 10; matrix products, arithmetic and copies ran while one was open for 1% -> 1% of each run, Pallas kernels for 13% -> 12%
where the time goes in v1:
time: 119 us; the launch traced here: 118 us
  starting transfers between devices  49.2 us (41%)
  waiting for transfers between devices  45.1 us (38%)
  Pallas kernels  19.5 us (16%)
  local copies, waits for them, and re-layouts  2.32 us (2%)
    ppermute x21, starting transfers between devices, shift_along(): return lax.ppermute(x, BLK_GRP, pairs)  40.4 us
    ppermute x21, waiting for transfers between devices, shift_along(): return lax.ppermute(x, BLK_GRP, pairs)  35.6 us
    all_to_all x1, waiting for transfers between devices, steps(): power = lax.all_to_all(terms, BLK_GRP, 0, 0, tiled=True)  9.12 us
    all_to_all x1, starting transfers between devices, steps(): power = lax.all_to_all(terms, BLK_GRP, 0, 0, tiled=True)  7.54 us
    pallas_call x3, Pallas kernels, chip_sums(): kernel_call(functools.partial(chip_sums_kernel, first, width, COLOURS[col...  6.71 us
    pallas_call x1, Pallas kernels, fourier_and_half(): kernel_call(functools.partial(fourier_kernel, first, width), 55, width *...  3.96 us
    pallas_call x1, Pallas kernels, later_halves(): kernel_call(halves_kernel, 48, 1 << 20, out_shape=[jax.ShapeDtypeStruct((...  2.9 us
    pallas_call x1, Pallas kernels, weights_and_own_half(): kernel_call(weights_kernel, 42, 1 << 26, out_shape=[jax.ShapeDtypeStruct(...  2.8 us
  transfers between devices with their start and end apart: 27, of which 10 were waited for; matrix products, arithmetic and copies ran while one was open for 1% of the time, Pallas kernels for 12%

profile of v1, /device:TPU:0, one launch (start us, length us, event | category | flops | bytes accessed | tf_op | source)
XLA Modules:
  0.0 118.0 jit_solution(10877839573537349268)
XLA Ops:
  0.7 4.0 %shard_map.59 = (bf16[256,128]{1,0:T(8,128)(2,1)}, bf16[256,128]{1,0:T(8,128)(2,1)}, bf16[4,512,512]{2,1,0:T(8,128)(2,1)}) custom-call(s32[1]{0:T(128)} %bitcast.core_ref, bf16[4,512,2048]{2,1,0:T(8,128)(2,1)} %leg_ref.5, f32[4,4,4096]{2,1,0:T(4,128)} %sky_ref.1, f32[320,128]{1,0:T(8,128)} %constant.117.clone.waves_ref), custom_call_target="tpu_custom_call" | custom-call | flops 4194304 | bytes 1048576 | tf_op jit(solution)/shard_map/pallas_call | solution.py:179
  5.2 2.9 %shard_map.60 = (bf16[4,512,256]{2,1,0:T(8,128)(2,1)}, bf16[4,512,256]{2,1,0:T(8,128)(2,1)}) custom-call(s32[1]{0:T(128)} %bitcast.core_ref, bf16[4,512,2048]{2,1,0:T(8,128)(2,1)} %leg_ref.5), custom_call_target="tpu_custom_call" | custom-call | flops 1048576 | bytes 1048576 | tf_op jit(solution)/shard_map/pallas_call | solution.py:82
  9.2 2.8 %shard_map.61 = (bf16[16,256,256]{2,1,0:T(8,128)(2,1)S(1)}, bf16[4,512,1024]{2,1,0:T(8,128)(2,1)S(1)}) custom-call(s32[1]{0:T(128)} %bitcast.core_ref, bf16[4,512,2048]{2,1,0:T(8,128)(2,1)} %leg_ref.5, bf16[256,128]{1,0:T(8,128)(2,1)S(1)} %copy-done, bf16[256,128]{1,0:T(8,128)(2,1)S(1)} %collective-permute-done.got_ref, ...), custom_call_target="tpu_custom_call" | custom-call | flops 67108864 | bytes 1048576 | tf_op jit(solution)/shard_map/pallas_call | solution.py:207
  12.0 2.4 %shard_map.62 = (bf16[128,8,512]{2,1,0:T(8,128)(2,1)S(1)}, bf16[128,8,512]{2,1,0:T(8,128)(2,1)S(1)}, bf16[128,8,512]{2,1,0:T(8,128)(2,1)S(1)}, bf16[128,8,512]{2,1,0:T(8,128)(2,1)S(1)}) custom-call(s32[4]{0:T(128)S(1)} %pad_add_fusion.1.here_ref, s32[512]{0:T(512)S(1)} %copy-done.1, bf16[16,256,256]{2,1,0:T(8,128)(2,1)S(1)} %get-tuple-element.44.weights, ...), custom_call_target="tpu_custom_call" | custom-call | flops 512000000 | bytes 1048576 | tf_op jit(solution)/shard_map/pallas_call | solution.py:266
  17.7 2.5 %shard_map.63 = (bf16[128,8,256]{2,1,0:T(8,128)(2,1)S(1)}, bf16[128,8,256]{2,1,0:T(8,128)(2,1)S(1)}, bf16[128,8,256]{2,1,0:T(8,128)(2,1)S(1)}, bf16[128,8,256]{2,1,0:T(8,128)(2,1)S(1)}) custom-call(s32[4]{0:T(128)S(1)} %pad_add_fusion.1.here_ref, s32[512]{0:T(512)S(1)} %copy-done.1, bf16[16,256,256]{2,1,0:T(8,128)(2,1)S(1)} %get-tuple-element.44.weights, ...), custom_call_target="tpu_custom_call" | custom-call | flops 256000000 | bytes 1048576 | tf_op jit(solution)/shard_map/pallas_call | solution.py:266
  21.9 1.8 %shard_map.64 = (bf16[128,8,256]{2,1,0:T(8,128)(2,1)S(1)}, bf16[128,8,256]{2,1,0:T(8,128)(2,1)S(1)}, bf16[128,8,256]{2,1,0:T(8,128)(2,1)S(1)}, bf16[128,8,256]{2,1,0:T(8,128)(2,1)S(1)}) custom-call(s32[4]{0:T(128)S(1)} %pad_add_fusion.1.here_ref, s32[512]{0:T(512)S(1)} %copy-done.1, bf16[16,256,256]{2,1,0:T(8,128)(2,1)S(1)} %get-tuple-element.44.weights, ...), custom_call_target="tpu_custom_call" | custom-call | flops 256000000 | bytes 1048576 | tf_op jit(solution)/shard_map/pallas_call | solution.py:266
  23.8 6.7 %collective-permute-done.3.b_ref = bf16[128,8,512]{2,1,0:T(8,128)(2,1)S(1)} collective-permute-done((bf16[128,8,512]{2,1,0:T(8,128)(2,1)S(1)}, bf16[128,8,512]{2,1,0:T(8,128)(2,1)S(1)}, u32[]{:S(2)}, u32[]{:S(2)}) %collective-permute-start.3) | collective-permute-done | bytes 1048608 | tf_op jit(solution)/shard_map/ppermute | solution.py:48
  32.7 3.8 %collective-permute-done.8.b_ref = bf16[128,8,256]{2,1,0:T(8,128)(2,1)S(1)} collective-permute-done((bf16[128,8,256]{2,1,0:T(8,128)(2,1)S(1)}, bf16[128,8,256]{2,1,0:T(8,128)(2,1)S(1)}, u32[]{:S(2)}, u32[]{:S(2)}) %collective-permute-start.8) | collective-permute-done | bytes 524320 | tf_op jit(solution)/shard_map/ppermute | solution.py:48
  36.6 2.9 %collective-permute-start.9 = (bf16[128,8,256]{2,1,0:T(8,128)(2,1)S(1)}, bf16[128,8,256]{2,1,0:T(8,128)(2,1)S(1)}, u32[]{:S(2)}, u32[]{:S(2)}) collective-permute-start(bf16[128,8,256]{2,1,0:T(8,128)(2,1)S(1)} %shard_map.66), channel_id=1, source_target_pairs={{0,96},{1,97},{2,26},{3,27},{4,100},{5,101},{6,30},{7,31},{8,104},... | collective-permute-start | bytes 1572872 | tf_op jit(solution)/shard_map/ppermute | solution.py:48
  39.5 4.0 %collective-permute-start.13 = (bf16[128,8,256]{2,1,0:T(8,128)(2,1)S(1)}, bf16[128,8,256]{2,1,0:T(8,128)(2,1)S(1)}, u32[]{:S(2)}, u32[]{:S(2)}) collective-permute-start(bf16[128,8,256]{2,1,0:T(8,128)(2,1)S(1)} %get-tuple-element.60), channel_id=1, source_target_pairs={{0,1},{1,0},{2,3},{3,2},{4,5},{5,4},{6,7},{7,6},{8,9},{9,8},{10,11... | collective-permute-start | bytes 1572872 | tf_op jit(solution)/shard_map/ppermute | solution.py:48
  43.5 8.9 %collective-permute-done.7.refs_4_ = bf16[128,8,256]{2,1,0:T(8,128)(2,1)S(1)} collective-permute-done((bf16[128,8,256]{2,1,0:T(8,128)(2,1)S(1)}, bf16[128,8,256]{2,1,0:T(8,128)(2,1)S(1)}, u32[]{:S(2)}, u32[]{:S(2)}) %collective-permute-start.7) | collective-permute-done | bytes 524320 | tf_op jit(solution)/shard_map/ppermute | solution.py:48
  52.4 2.0 %collective-permute-start.14 = (bf16[128,8,256]{2,1,0:T(8,128)(2,1)S(1)}, bf16[128,8,256]{2,1,0:T(8,128)(2,1)S(1)}, u32[]{:S(2)}, u32[]{:S(2)}) collective-permute-start(bf16[128,8,256]{2,1,0:T(8,128)(2,1)S(1)} %get-tuple-element.61), channel_id=1, source_target_pairs={{0,4},{1,5},{2,6},{3,7},{4,1},{5,0},{6,3},{7,2},{8,12},{9,13},{10,... | collective-permute-start | bytes 1572872 | tf_op jit(solution)/shard_map/ppermute | solution.py:48
  54.4 2.1 %collective-permute-start.15 = (bf16[128,8,256]{2,1,0:T(8,128)(2,1)S(1)}, bf16[128,8,256]{2,1,0:T(8,128)(2,1)S(1)}, u32[]{:S(2)}, u32[]{:S(2)}) collective-permute-start(bf16[128,8,256]{2,1,0:T(8,128)(2,1)S(1)} %get-tuple-element.62), channel_id=1, source_target_pairs={{0,5},{1,4},{2,7},{3,6},{4,0},{5,1},{6,2},{7,3},{8,13},{9,12},{10,... | collective-permute-start | bytes 1572872 | tf_op jit(solution)/shard_map/ppermute | solution.py:48
  57.6 3.2 %collective-permute-start.10 = (bf16[32,8,768]{2,1,0:T(8,128)(2,1)S(1)}, bf16[32,8,768]{2,1,0:T(8,128)(2,1)S(1)}, u32[]{:S(2)}, u32[]{:S(2)}) collective-permute-start(bf16[32,8,768]{2,1,0:T(8,128)(2,1)S(1)} %get-tuple-element.57), channel_id=1, source_target_pairs={{0,16},{1,17},{2,3},{3,2},{4,20},{5,21},{6,7},{7,6},{8,24},{9,25},... | collective-permute-start | bytes 1179656 | tf_op jit(solution)/shard_map/ppermute | solution.py:48
  61.5 2.6 %collective-permute-start.12 = (bf16[32,8,768]{2,1,0:T(8,128)(2,1)S(1)}, bf16[32,8,768]{2,1,0:T(8,128)(2,1)S(1)}, u32[]{:S(2)}, u32[]{:S(2)}) collective-permute-start(bf16[32,8,768]{2,1,0:T(8,128)(2,1)S(1)} %get-tuple-element.59), channel_id=1, source_target_pairs={{0,24},{1,25},{2,7},{3,6},{4,28},{5,29},{6,2},{7,3},{8,0},{9,1},{1... | collective-permute-start | bytes 1179656 | tf_op jit(solution)/shard_map/ppermute | solution.py:48
  64.0 9.5 %collective-permute-done.14.refs_2_ = bf16[128,8,256]{2,1,0:T(8,128)(2,1)S(1)} collective-permute-done((bf16[128,8,256]{2,1,0:T(8,128)(2,1)S(1)}, bf16[128,8,256]{2,1,0:T(8,128)(2,1)S(1)}, u32[]{:S(2)}, u32[]{:S(2)}) %collective-permute-start.14) | collective-permute-done | bytes 524320 | tf_op jit(solution)/shard_map/ppermute | solution.py:48
  75.0 2.5 %collective-permute-start.21 = (bf16[32,8,256]{2,1,0:T(8,128)(2,1)S(1)}, bf16[32,8,256]{2,1,0:T(8,128)(2,1)S(1)}, u32[]{:S(2)}, u32[]{:S(2)}) collective-permute-start(bf16[32,8,256]{2,1,0:T(8,128)(2,1)S(1)} %get-tuple-element.70), channel_id=1, source_target_pairs={{0,96},{1,97},{2,98},{3,99},{4,100},{5,101},{6,102},{7,103},{8,104... | collective-permute-start | bytes 393224 | tf_op jit(solution)/shard_map/ppermute | solution.py:48
  77.7 3.4 %collective-permute-done.19.refs_1_ = bf16[32,8,256]{2,1,0:T(8,128)(2,1)S(1)} collective-permute-done((bf16[32,8,256]{2,1,0:T(8,128)(2,1)}, bf16[32,8,256]{2,1,0:T(8,128)(2,1)S(1)}, u32[]{:S(2)}, u32[]{:S(2)}) %collective-permute-start.19) | collective-permute-done | bytes 131104 | tf_op jit(solution)/shard_map/ppermute | solution.py:48
  82.0 3.3 %collective-permute-start.22 = (bf16[8,8,256]{2,1,0:T(8,128)(2,1)S(1)}, bf16[8,8,256]{2,1,0:T(8,128)(2,1)S(1)}, u32[]{:S(2)}, u32[]{:S(2)}) collective-permute-start(bf16[8,8,256]{2,1,0:T(8,128)(2,1)S(1)} %get-tuple-element.72), channel_id=1, source_target_pairs={{0,16},{1,17},{2,18},{3,19},{4,20},{5,21},{6,22},{7,23},{8,24},{9,... | collective-permute-start | bytes 98312 | tf_op jit(solution)/shard_map/ppermute | solution.py:48
  85.4 2.9 %collective-permute-start.16 = (bf16[8,8,768]{2,1,0:T(8,128)(2,1)S(1)}, bf16[8,8,768]{2,1,0:T(8,128)(2,1)S(1)}, u32[]{:S(2)}, u32[]{:S(2)}) collective-permute-start(bf16[8,8,768]{2,1,0:T(8,128)(2,1)S(1)} %get-tuple-element.65), channel_id=1, source_target_pairs={{0,1},{1,0},{2,66},{3,67},{4,5},{5,4},{6,70},{7,71},{8,9},{9,8},{1... | collective-permute-start | bytes 294920 | tf_op jit(solution)/shard_map/ppermute | solution.py:48
  89.2 2.3 %collective-permute-start.18 = (bf16[8,8,768]{2,1,0:T(8,128)(2,1)S(1)}, bf16[8,8,768]{2,1,0:T(8,128)(2,1)S(1)}, u32[]{:S(2)}, u32[]{:S(2)}) collective-permute-start(bf16[8,8,768]{2,1,0:T(8,128)(2,1)S(1)} %get-tuple-element.67), channel_id=1, source_target_pairs={{0,5},{1,4},{2,98},{3,99},{4,0},{5,1},{6,102},{7,103},{8,13},{9,12... | collective-permute-start | bytes 294920 | tf_op jit(solution)/shard_map/ppermute | solution.py:48
  91.5 1.8 %collective-permute-start.23 = (bf16[8,8,256]{2,1,0:T(8,128)(2,1)S(1)}, bf16[8,8,256]{2,1,0:T(8,128)(2,1)S(1)}, u32[]{:S(2)}, u32[]{:S(2)}) collective-permute-start(bf16[8,8,256]{2,1,0:T(8,128)(2,1)S(1)} %get-tuple-element.73), channel_id=1, source_target_pairs={{0,8},{1,9},{2,10},{3,11},{4,12},{5,13},{6,14},{7,15},{8,16},{9,17... | collective-permute-start | bytes 98312 | tf_op jit(solution)/shard_map/ppermute | solution.py:48
  99.5 7.5 %all-to-all-start = ((f32[128,1,160]{2,1,0:T(1,128)}), f32[128,1,160]{2,1,0:T(1,128)S(1)}, u32[]{:S(2)}, u32[]{:S(2)}) async-start(f32[128,1,160]{2,1,0:T(1,128)} %copy.10), calls=%async_computation | async-start | bytes 262144 | tf_op jit(solution)/shard_map/all_to_all | solution.py:427
  107.1 9.1 %all-to-all-done = f32[128,1,160]{2,1,0:T(1,128)S(1)} async-done(((f32[128,1,160]{2,1,0:T(1,128)}), f32[128,1,160]{2,1,0:T(1,128)S(1)}, u32[]{:S(2)}, u32[]{:S(2)}) %all-to-all-start) | async-done | bytes 81952 | tf_op jit(solution)/shard_map/all_to_all | solution.py:427
  (64 shorter events, 22.1 us)
Async XLA Ops:
  4.6 7.4 %collective-permute-start.1 = (bf16[4,512,512]{2,1,0:T(8,128)(2,1)}, bf16[4,512,512]{2,1,0:T(8,128)(2,1)S(1)}, u32[]{:S(2)}, u32[]{:S(2)}) collective-permute-start(bf16[4,512,512]{2,1,0:T(8,128)(2,1)} %get-tuple-element.46), channel_id=1, source_target_pairs={{0,2},{2,0},{1,3},{3,1},{4,6},{6,4},{5,7},{7,5},{8,10},{10,8},{9,1... | collective-permute-start | bytes 6291464 | tf_op jit(solution)/shard_map/ppermute | solution.py:52
  8.1 13.8 %collective-permute-start.4 = (bf16[4,512,256]{2,1,0:T(8,128)(2,1)}, bf16[4,512,256]{2,1,0:T(8,128)(2,1)S(1)}, u32[]{:S(2)}, u32[]{:S(2)}) collective-permute-start(bf16[4,512,256]{2,1,0:T(8,128)(2,1)} %get-tuple-element.43.rest_1_), channel_id=1, source_target_pairs={{0,2},{2,0},{1,3},{3,1},{4,6},{6,4},{5,7},{7,5},{8,10},{10,8},{9,1... | collective-permute-start | bytes 3145736 | tf_op jit(solution)/shard_map/ppermute | solution.py:52
  8.3 9.4 %collective-permute-start.5 = (bf16[4,512,256]{2,1,0:T(8,128)(2,1)}, bf16[4,512,256]{2,1,0:T(8,128)(2,1)}, u32[]{:S(2)}, u32[]{:S(2)}) collective-permute-start(bf16[4,512,256]{2,1,0:T(8,128)(2,1)} %get-tuple-element.42.rest_0_), channel_id=1, source_target_pairs={{0,2},{2,0},{1,3},{3,1},{4,6},{6,4},{5,7},{7,5},{8,10},{10,8},{9,1... | collective-permute-start | bytes 3145736 | tf_op jit(solution)/shard_map/ppermute | solution.py:52
  14.4 16.1 %collective-permute-start.3 = (bf16[128,8,512]{2,1,0:T(8,128)(2,1)S(1)}, bf16[128,8,512]{2,1,0:T(8,128)(2,1)S(1)}, u32[]{:S(2)}, u32[]{:S(2)}) collective-permute-start(bf16[128,8,512]{2,1,0:T(8,128)(2,1)S(1)} %get-tuple-element.50), channel_id=1, source_target_pairs={{0,32},{1,33},{2,10},{3,11},{4,36},{5,37},{6,14},{7,15},{8,40},{9,... | collective-permute-start | bytes 3145736 | tf_op jit(solution)/shard_map/ppermute | solution.py:48
  16.1 38.4 %collective-permute-start.2 = (bf16[128,8,512]{2,1,0:T(8,128)(2,1)S(1)}, bf16[128,8,512]{2,1,0:T(8,128)(2,1)S(1)}, u32[]{:S(2)}, u32[]{:S(2)}) collective-permute-start(bf16[128,8,512]{2,1,0:T(8,128)(2,1)S(1)} %get-tuple-element.48), channel_id=1, source_target_pairs={{0,96},{1,97},{2,26},{3,27},{4,100},{5,101},{6,30},{7,31},{8,104},... | collective-permute-start | bytes 3145736 | tf_op jit(solution)/shard_map/ppermute | solution.py:48
  20.2 16.3 %collective-permute-start.8 = (bf16[128,8,256]{2,1,0:T(8,128)(2,1)S(1)}, bf16[128,8,256]{2,1,0:T(8,128)(2,1)S(1)}, u32[]{:S(2)}, u32[]{:S(2)}) collective-permute-start(bf16[128,8,256]{2,1,0:T(8,128)(2,1)S(1)} %get-tuple-element.55), channel_id=1, source_target_pairs={{0,96},{1,97},{2,26},{3,27},{4,100},{5,101},{6,30},{7,31},{8,104},... | collective-permute-start | bytes 1572872 | tf_op jit(solution)/shard_map/ppermute | solution.py:48
  30.7 25.9 %collective-permute-start.6 = (bf16[128,8,512]{2,1,0:T(8,128)(2,1)S(1)}, bf16[128,8,512]{2,1,0:T(8,128)(2,1)S(1)}, u32[]{:S(2)}, u32[]{:S(2)}) collective-permute-start(bf16[128,8,512]{2,1,0:T(8,128)(2,1)S(1)} %shard_map.65.rest_0_), channel_id=1, source_target_pairs={{0,32},{1,33},{2,10},{3,11},{4,36},{5,37},{6,14},{7,15},{8,40},{9,... | collective-permute-start | bytes 3145736 | tf_op jit(solution)/shard_map/ppermute | solution.py:48
  31.2 21.2 %collective-permute-start.7 = (bf16[128,8,256]{2,1,0:T(8,128)(2,1)S(1)}, bf16[128,8,256]{2,1,0:T(8,128)(2,1)S(1)}, u32[]{:S(2)}, u32[]{:S(2)}) collective-permute-start(bf16[128,8,256]{2,1,0:T(8,128)(2,1)S(1)} %get-tuple-element.53), channel_id=1, source_target_pairs={{0,32},{1,33},{2,10},{3,11},{4,36},{5,37},{6,14},{7,15},{8,40},{9,... | collective-permute-start | bytes 1572872 | tf_op jit(solution)/shard_map/ppermute | solution.py:48
  36.6 20.0 %collective-permute-start.9 = (bf16[128,8,256]{2,1,0:T(8,128)(2,1)S(1)}, bf16[128,8,256]{2,1,0:T(8,128)(2,1)S(1)}, u32[]{:S(2)}, u32[]{:S(2)}) collective-permute-start(bf16[128,8,256]{2,1,0:T(8,128)(2,1)S(1)} %shard_map.66), channel_id=1, source_target_pairs={{0,96},{1,97},{2,26},{3,27},{4,100},{5,101},{6,30},{7,31},{8,104},... | collective-permute-start | bytes 1572872 | tf_op jit(solution)/shard_map/ppermute | solution.py:48
  39.5 21.9 %collective-permute-start.13 = (bf16[128,8,256]{2,1,0:T(8,128)(2,1)S(1)}, bf16[128,8,256]{2,1,0:T(8,128)(2,1)S(1)}, u32[]{:S(2)}, u32[]{:S(2)}) collective-permute-start(bf16[128,8,256]{2,1,0:T(8,128)(2,1)S(1)} %get-tuple-element.60), channel_id=1, source_target_pairs={{0,1},{1,0},{2,3},{3,2},{4,5},{5,4},{6,7},{7,6},{8,9},{9,8},{10,11... | collective-permute-start | bytes 1572872 | tf_op jit(solution)/shard_map/ppermute | solution.py:48
  52.4 21.1 %collective-permute-start.14 = (bf16[128,8,256]{2,1,0:T(8,128)(2,1)S(1)}, bf16[128,8,256]{2,1,0:T(8,128)(2,1)S(1)}, u32[]{:S(2)}, u32[]{:S(2)}) collective-permute-start(bf16[128,8,256]{2,1,0:T(8,128)(2,1)S(1)} %get-tuple-element.61), channel_id=1, source_target_pairs={{0,4},{1,5},{2,6},{3,7},{4,1},{5,0},{6,3},{7,2},{8,12},{9,13},{10,... | collective-permute-start | bytes 1572872 | tf_op jit(solution)/shard_map/ppermute | solution.py:48
  54.4 19.1 %collective-permute-start.15 = (bf16[128,8,256]{2,1,0:T(8,128)(2,1)S(1)}, bf16[128,8,256]{2,1,0:T(8,128)(2,1)S(1)}, u32[]{:S(2)}, u32[]{:S(2)}) collective-permute-start(bf16[128,8,256]{2,1,0:T(8,128)(2,1)S(1)} %get-tuple-element.62), channel_id=1, source_target_pairs={{0,5},{1,4},{2,7},{3,6},{4,0},{5,1},{6,2},{7,3},{8,13},{9,12},{10,... | collective-permute-start | bytes 1572872 | tf_op jit(solution)/shard_map/ppermute | solution.py:48
  57.6 17.5 %collective-permute-start.10 = (bf16[32,8,768]{2,1,0:T(8,128)(2,1)S(1)}, bf16[32,8,768]{2,1,0:T(8,128)(2,1)S(1)}, u32[]{:S(2)}, u32[]{:S(2)}) collective-permute-start(bf16[32,8,768]{2,1,0:T(8,128)(2,1)S(1)} %get-tuple-element.57), channel_id=1, source_target_pairs={{0,16},{1,17},{2,3},{3,2},{4,20},{5,21},{6,7},{7,6},{8,24},{9,25},... | collective-permute-start | bytes 1179656 | tf_op jit(solution)/shard_map/ppermute | solution.py:48
  60.8 16.8 %collective-permute-start.11 = (bf16[32,8,768]{2,1,0:T(8,128)(2,1)}, bf16[32,8,768]{2,1,0:T(8,128)(2,1)S(1)}, u32[]{:S(2)}, u32[]{:S(2)}) collective-permute-start(bf16[32,8,768]{2,1,0:T(8,128)(2,1)} %get-tuple-element.58), channel_id=1, source_target_pairs={{0,8},{1,9},{2,6},{3,7},{4,12},{5,13},{6,3},{7,2},{8,16},{9,17},{1... | collective-permute-start | bytes 1179656 | tf_op jit(solution)/shard_map/ppermute | solution.py:48
  61.5 16.1 %collective-permute-start.12 = (bf16[32,8,768]{2,1,0:T(8,128)(2,1)S(1)}, bf16[32,8,768]{2,1,0:T(8,128)(2,1)S(1)}, u32[]{:S(2)}, u32[]{:S(2)}) collective-permute-start(bf16[32,8,768]{2,1,0:T(8,128)(2,1)S(1)} %get-tuple-element.59), channel_id=1, source_target_pairs={{0,24},{1,25},{2,7},{3,6},{4,28},{5,29},{6,2},{7,3},{8,0},{9,1},{1... | collective-permute-start | bytes 1179656 | tf_op jit(solution)/shard_map/ppermute | solution.py:48
  74.3 6.8 %collective-permute-start.19 = (bf16[32,8,256]{2,1,0:T(8,128)(2,1)}, bf16[32,8,256]{2,1,0:T(8,128)(2,1)S(1)}, u32[]{:S(2)}, u32[]{:S(2)}) collective-permute-start(bf16[32,8,256]{2,1,0:T(8,128)(2,1)} %get-tuple-element.68), channel_id=1, source_target_pairs={{0,64},{1,65},{2,66},{3,67},{4,68},{5,69},{6,70},{7,71},{8,72},{9,... | collective-permute-start | bytes 393224 | tf_op jit(solution)/shard_map/ppermute | solution.py:48
  74.3 7.6 %collective-permute-start.20 = (bf16[32,8,256]{2,1,0:T(8,128)(2,1)S(1)}, bf16[32,8,256]{2,1,0:T(8,128)(2,1)S(1)}, u32[]{:S(2)}, u32[]{:S(2)}) collective-permute-start(bf16[32,8,256]{2,1,0:T(8,128)(2,1)S(1)} %get-tuple-element.69), channel_id=1, source_target_pairs={{0,32},{1,33},{2,34},{3,35},{4,36},{5,37},{6,38},{7,39},{8,40},{9,... | collective-permute-start | bytes 393224 | tf_op jit(solution)/shard_map/ppermute | solution.py:48
  75.0 6.9 %collective-permute-start.21 = (bf16[32,8,256]{2,1,0:T(8,128)(2,1)S(1)}, bf16[32,8,256]{2,1,0:T(8,128)(2,1)S(1)}, u32[]{:S(2)}, u32[]{:S(2)}) collective-permute-start(bf16[32,8,256]{2,1,0:T(8,128)(2,1)S(1)} %get-tuple-element.70), channel_id=1, source_target_pairs={{0,96},{1,97},{2,98},{3,99},{4,100},{5,101},{6,102},{7,103},{8,104... | collective-permute-start | bytes 393224 | tf_op jit(solution)/shard_map/ppermute | solution.py:48
  82.0 11.4 %collective-permute-start.22 = (bf16[8,8,256]{2,1,0:T(8,128)(2,1)S(1)}, bf16[8,8,256]{2,1,0:T(8,128)(2,1)S(1)}, u32[]{:S(2)}, u32[]{:S(2)}) collective-permute-start(bf16[8,8,256]{2,1,0:T(8,128)(2,1)S(1)} %get-tuple-element.72), channel_id=1, source_target_pairs={{0,16},{1,17},{2,18},{3,19},{4,20},{5,21},{6,22},{7,23},{8,24},{9,... | collective-permute-start | bytes 98312 | tf_op jit(solution)/shard_map/ppermute | solution.py:48
  85.4 11.9 %collective-permute-start.16 = (bf16[8,8,768]{2,1,0:T(8,128)(2,1)S(1)}, bf16[8,8,768]{2,1,0:T(8,128)(2,1)S(1)}, u32[]{:S(2)}, u32[]{:S(2)}) collective-permute-start(bf16[8,8,768]{2,1,0:T(8,128)(2,1)S(1)} %get-tuple-element.65), channel_id=1, source_target_pairs={{0,1},{1,0},{2,66},{3,67},{4,5},{5,4},{6,70},{7,71},{8,9},{9,8},{1... | collective-permute-start | bytes 294920 | tf_op jit(solution)/shard_map/ppermute | solution.py:48
  88.3 9.0 %collective-permute-start.17 = (bf16[8,8,768]{2,1,0:T(8,128)(2,1)S(1)}, bf16[8,8,768]{2,1,0:T(8,128)(2,1)S(1)}, u32[]{:S(2)}, u32[]{:S(2)}) collective-permute-start(bf16[8,8,768]{2,1,0:T(8,128)(2,1)S(1)} %get-tuple-element.66), channel_id=1, source_target_pairs={{0,4},{1,5},{2,34},{3,35},{4,1},{5,0},{6,38},{7,39},{8,12},{9,13},... | collective-permute-start | bytes 294920 | tf_op jit(solution)/shard_map/ppermute | solution.py:48
  89.2 8.1 %collective-permute-start.18 = (bf16[8,8,768]{2,1,0:T(8,128)(2,1)S(1)}, bf16[8,8,768]{2,1,0:T(8,128)(2,1)S(1)}, u32[]{:S(2)}, u32[]{:S(2)}) collective-permute-start(bf16[8,8,768]{2,1,0:T(8,128)(2,1)S(1)} %get-tuple-element.67), channel_id=1, source_target_pairs={{0,5},{1,4},{2,98},{3,99},{4,0},{5,1},{6,102},{7,103},{8,13},{9,12... | collective-permute-start | bytes 294920 | tf_op jit(solution)/shard_map/ppermute | solution.py:48
  99.5 16.8 %all-to-all-start = ((f32[128,1,160]{2,1,0:T(1,128)}), f32[128,1,160]{2,1,0:T(1,128)S(1)}, u32[]{:S(2)}, u32[]{:S(2)}) async-start(f32[128,1,160]{2,1,0:T(1,128)} %copy.10), calls=%async_computation | async-start | bytes 262144 | tf_op jit(solution)/shard_map/all_to_all | solution.py:427
  107.0 10.1 %collective-permute-start.25 = (f32[4,8,1024]{2,1,0:T(8,128)S(1)}, f32[4,8,1024]{2,1,0:T(8,128)S(1)}, u32[]{:S(2)}, u32[]{:S(2)}) collective-permute-start(f32[4,8,1024]{2,1,0:T(8,128)S(1)} %get-tuple-element.76), channel_id=1, source_target_pairs={{0,2},{2,0},{1,3},{3,1},{4,6},{6,4},{5,7},{7,5},{8,10},{10,8},{9,1... | collective-permute-start | bytes 393224 | tf_op jit(solution)/shard_map/ppermute | solution.py:52
  (5 other events, 20.8 us)

commit v2 on v1

--- a/solution.py
+++ b/solution.py
@@ -66,27 +66,21 @@
     return pltpu.make_async_copy(leg_ref.at[:, :, pl.ds(start, width)], out_ref, sem)
 
 
-def halves_kernel(core_ref, leg_ref, *rest):
-    outs, sems = rest[:-1], rest[-1]
-    copies = [
-        half_copy(first, width, core_ref, leg_ref, out, sems.at[k])
-        for k, ((first, width, _), out) in enumerate(zip(PIECES[1:], outs))
-    ]
-    for copy in copies:
-        copy.start()
-    for copy in copies:
-        copy.wait()
-
-
-def later_halves(core, legendre):
-    return kernel_call(
-        halves_kernel,
-        48,
+def half_kernel(core_ref, leg_ref, out_ref, sem):
+    copy = half_copy(*PIECES[1][:2], core_ref, leg_ref, out_ref, sem)
+    copy.start()
+    copy.wait()
+
+
+def second_half(core, legendre):
+    return kernel_call(
+        half_kernel,
+        50,
         1 << 20,
-        out_shape=[jax.ShapeDtypeStruct((4, 512, width), BF16) for _, width, _ in PIECES[1:]],
+        out_shape=jax.ShapeDtypeStruct((4, 512, PIECES[1][1]), BF16),
         in_specs=[SMEM, HBM],
-        out_specs=[VMEM] * len(PIECES[1:]),
-        scratch_shapes=[pltpu.SemaphoreType.DMA((len(PIECES) - 1,))],
+        out_specs=VMEM,
+        scratch_shapes=[pltpu.SemaphoreType.DMA],
     )(core, legendre)
 
 
@@ -128,9 +122,10 @@
 
 
 def fourier_kernel(
-    first, width, core_ref, leg_ref, sky_ref, waves_ref, out_ref, send_ref, half_ref, x_ref, cos_ref, sin_ref, tail_ref, z_ref, sems
+    core_ref, leg_ref, sky_ref, waves_ref, out_ref, send_ref, half_ref, last_ref, x_ref, cos_ref, sin_ref, tail_ref, z_ref, sems
 ):
-    half = half_copy(first, width, core_ref, leg_ref, half_ref, sems.at[0])
+    half = half_copy(*PIECES[0][:2], core_ref, leg_ref, half_ref, sems.at[0])
+    last = half_copy(*PIECES[2][:2], core_ref, leg_ref, last_ref, sems.at[5])
     copies = [
         pltpu.make_async_copy(sky_ref, x_ref, sems.at[1]),
         pltpu.make_async_copy(waves_ref.at[0:32], cos_ref, sems.at[2]),
@@ -140,6 +135,7 @@
     for copy in copies:
         copy.start()
     half.start()
+    last.start()
     for copy in copies:
         copy.wait()
     row = lax.broadcasted_iota(jnp.int32, (8, 128), 0)
@@ -167,9 +163,10 @@
     out_ref[...] = rounded
     send_ref[...] = rounded
     half.wait()
-
-
-def fourier_and_half(first, width, core, legendre, sky_maps):
+    last.wait()
+
+
+def fourier_and_half(core, legendre, sky_maps):
     turn = 2 * np.pi / 4096 * np.outer(np.arange(32), np.arange(128))
     last = 2 * np.pi / 128 * np.outer(np.arange(128), np.arange(16))
     tail = np.zeros((256, 128))
@@ -177,19 +174,20 @@
     tail[128:, :16] = np.sin(last)
     waves = np.concatenate([np.cos(turn), np.sin(turn), tail])
     return kernel_call(
-        functools.partial(fourier_kernel, first, width),
+        fourier_kernel,
         55,
-        width * 8192,
-        out_shape=[jax.ShapeDtypeStruct((256, 128), BF16)] * 2 + [jax.ShapeDtypeStruct((4, 512, width), BF16)],
+        1 << 22,
+        out_shape=[jax.ShapeDtypeStruct((256, 128), BF16)] * 2
+        + [jax.ShapeDtypeStruct((4, 512, PIECES[k][1]), BF16) for k in (0, 2)],
         in_specs=[SMEM] + [HBM] * 3,
-        out_specs=[VMEM] * 3,
+        out_specs=[VMEM] * 4,
         scratch_shapes=[
             pltpu.VMEM((4, 4, 4096), F32),
             pltpu.VMEM((32, 128), F32),
             pltpu.VMEM((32, 128), F32),
             pltpu.VMEM((256, 128), F32),
             pltpu.VMEM((256, 256), F32),
-            pltpu.SemaphoreType.DMA((5,)),
+            pltpu.SemaphoreType.DMA((6,)),
         ],
     )(core, legendre, sky_maps, jnp.asarray(waves, F32))
 
@@ -346,11 +344,14 @@
         for j in range(4):
             own_ref[j, :, lane] = slot_sum(core * 4 + j)
             send_ref[j, :, lane] = slot_sum((1 - core) * 4 + j)
+        here = pl.ds(pl.multiple_of(core * 1024 + first, 128), width)
+        there = pl.ds(pl.multiple_of((1 - core) * 1024 + first, 128), width)
+        cross_ref[:, there] = jnp.zeros((10, width), F32)
         row = 0
         for i in range(4):
             for j in range(i, 4):
                 t = totals[j - i]
-                cross_ref[row : row + 1, lane] = t[2 * i : 2 * i + 1] + t[2 * i + 1 : 2 * i + 2]
+                cross_ref[row : row + 1, here] = t[2 * i : 2 * i + 1] + t[2 * i + 1 : 2 * i + 2]
                 row += 1
 
 
@@ -362,7 +363,7 @@
         out_shape=[
             jax.ShapeDtypeStruct((4, 8, 1024), F32),
             jax.ShapeDtypeStruct((4, 8, 1024), F32),
-            jax.ShapeDtypeStruct((10, 1024), F32),
+            jax.ShapeDtypeStruct((10, 2048), F32),
         ],
         in_specs=[SMEM, SMEM] + [VMEM] * len(parts),
         out_specs=[VMEM] * 3,
@@ -377,12 +378,13 @@
 
     here_scalars = jnp.stack([here[axis] for axis in (X, Y, Z, CORE)]).astype(jnp.int32)
 
-    own_f, send_f, half = fourier_and_half(*PIECES[0][:2], core_scalar, legendre, sky_maps)
+    own_f, send_f, half, half_2 = fourier_and_half(core_scalar, legendre, sky_maps)
     got_f = swap_cores(send_f)
     got_0 = swap_cores(half)
-    half_1, half_2 = later_halves(core_scalar, legendre)
-    got_1, got_2 = swap_cores(half_1), swap_cores(half_2)
-    weights, table = weights_and_own_half(core_scalar, legendre, own_f, got_f, half_1, half_2)
+    half_1 = second_half(core_scalar, legendre)
+    got_1 = swap_cores(half_1)
+    got_2 = swap_cores(half_2)
+    weights, table = weights_and_own_half(core_scalar, legendre, own_f, got_f, half_1)
 
     def move(block, stage, colour, shift):
         axes = COLOURS[colour][2]
@@ -399,9 +401,10 @@
     down = sums_of(1, got_1)
     through_down, from_below = move(down[2], 0, 0, 3), move(down[1], 0, 0, 1)
     sent = sums_of(2, got_2, down[0])
-    colour_1 = [exchange(sent, 0, 1)]
+    colour_1 = [[sent[0], move(sent[2], 0, 1, 2)]]
     both_up = combine(up[1], through_up, sent[0])
     from_below_up = move(both_up, 0, 0, 1)
+    colour_1[0] += [move(sent[d], 0, 1, d) for d in (1, 3)]
     both_down = combine(down[3], through_down, both_up)
     from_above_down = move(both_down, 0, 0, 3)
     colour_0 = [[up[0], from_above, from_below_up], [down[0], from_below, from_above_down]]
@@ -421,9 +424,7 @@
     own, send, cross = finish(core_scalar, chip_orders, last)
     got = swap_cores(send)
 
-    terms = jnp.transpose(cross.reshape(10, 64, 16), (1, 0, 2)).reshape(64, 160)
-    nothing = jnp.zeros_like(terms)
-    terms = jnp.concatenate([jnp.where(core == 0, terms, nothing), jnp.where(core == 1, terms, nothing)])
+    terms = jnp.transpose(cross.reshape(10, 128, 16), (1, 0, 2)).reshape(128, 160)
     power = lax.all_to_all(terms, BLK_GRP, 0, 0, tiled=True)
     power = jnp.sum(power, axis=0).reshape(10, 16)
     ells = my_index * 16 + lax.iota(jnp.int32, 16)

time: 119 us -> 119 us (level)
    ppermute x5, waiting for transfers between devices: 0.39 us -> 2.05 us  [swap_cores(): return lax.ppermute(x, CORE, [(0, 1), (1, 0)])]
    pallas_call x2, Pallas kernels: 6.86 us -> 5.52 us  [the longest x1 4.29 us: fourier_and_half(): kernel_call(fourier_kernel, 55, 1 << 22, out_shape=[jax.ShapeDtypeStruct(...]
where the time goes in v2:
time: 119 us; the launch traced here: 118 us
  starting transfers between devices  49.2 us (41%)
  waiting for transfers between devices  46.1 us (39%)
  Pallas kernels  18.8 us (16%)
  local copies, waits for them, and re-layouts  2.21 us (2%)
    ppermute x21, starting transfers between devices, shift_along(): return lax.ppermute(x, BLK_GRP, pairs)  40.4 us
    ppermute x21, waiting for transfers between devices, shift_along(): return lax.ppermute(x, BLK_GRP, pairs)  34.9 us
    all_to_all x1, waiting for transfers between devices, steps(): power = lax.all_to_all(terms, BLK_GRP, 0, 0, tiled=True)  9.12 us
    all_to_all x1, starting transfers between devices, steps(): power = lax.all_to_all(terms, BLK_GRP, 0, 0, tiled=True)  7.54 us
    pallas_call x3, Pallas kernels, chip_sums(): kernel_call(functools.partial(chip_sums_kernel, first, width, COLOURS[col...  7.38 us
    pallas_call x1, Pallas kernels, fourier_and_half(): kernel_call(fourier_kernel, 55, 1 << 22, out_shape=[jax.ShapeDtypeStruct(...  4.29 us
    pallas_call x1, Pallas kernels, weights_and_own_half(): kernel_call(weights_kernel, 42, 1 << 26, out_shape=[jax.ShapeDtypeStruct(...  2.8 us
  transfers between devices with their start and end apart: 27, of which 10 were waited for; matrix products, arithmetic and copies ran while one was open for 1% of the time, Pallas kernels for 12%

profile of v2, /device:TPU:0, one launch (start us, length us, event | category | flops | bytes accessed | tf_op | source)
XLA Modules:
  0.0 118.1 jit_solution(195095998600687233)
XLA Ops:
  0.7 4.3 %shard_map.59 = (bf16[256,128]{1,0:T(8,128)(2,1)}, bf16[256,128]{1,0:T(8,128)(2,1)}, bf16[4,512,512]{2,1,0:T(8,128)(2,1)}, bf16[4,512,256]{2,1,0:T(8,128)(2,1)}) custom-call(s32[1]{0:T(128)} %bitcast.core_ref, bf16[4,512,2048]{2,1,0:T(8,128)(2,1)} %leg_ref.5, f32[4,4,4096]{2,1,0:T(4,128)} %sky_ref.1, f32[320,128]{1,0:T(8,128)} %constant.115.clone.waves_ref), custom_call_target="tpu_custom_call" | custom-call | flops 4194304 | bytes 1048576 | tf_op jit(solution)/shard_map/pallas_call | solution.py:176
  7.5 2.0 %collective-permute-done.got_ref = bf16[256,128]{1,0:T(8,128)(2,1)S(1)} collective-permute-done((bf16[256,128]{1,0:T(8,128)(2,1)}, bf16[256,128]{1,0:T(8,128)(2,1)S(1)}, u32[]{:S(2)}, u32[]{:S(2)}) %collective-permute-start) | collective-permute-done | bytes 65568 | tf_op jit(solution)/shard_map/ppermute | solution.py:52
  9.5 2.8 %shard_map.61 = (bf16[16,256,256]{2,1,0:T(8,128)(2,1)S(1)}, bf16[4,512,1024]{2,1,0:T(8,128)(2,1)S(1)}) custom-call(s32[1]{0:T(128)} %bitcast.core_ref, bf16[4,512,2048]{2,1,0:T(8,128)(2,1)} %leg_ref.5, bf16[256,128]{1,0:T(8,128)(2,1)S(1)} %copy-done, bf16[256,128]{1,0:T(8,128)(2,1)S(1)} %collective-permute-done.got_ref, ...), custom_call_target="tpu_custom_call" | custom-call | flops 67108864 | bytes 1048576 | tf_op jit(solution)/shard_map/pallas_call | solution.py:205
  12.3 2.4 %shard_map.62 = (bf16[128,8,512]{2,1,0:T(8,128)(2,1)S(1)}, bf16[128,8,512]{2,1,0:T(8,128)(2,1)S(1)}, bf16[128,8,512]{2,1,0:T(8,128)(2,1)S(1)}, bf16[128,8,512]{2,1,0:T(8,128)(2,1)S(1)}) custom-call(s32[4]{0:T(128)S(1)} %pad_add_fusion.1.here_ref, s32[512]{0:T(512)S(1)} %copy-done.1, bf16[16,256,256]{2,1,0:T(8,128)(2,1)S(1)} %get-tuple-element.41.weights, ...), custom_call_target="tpu_custom_call" | custom-call | flops 512000000 | bytes 1048576 | tf_op jit(solution)/shard_map/pallas_call | solution.py:264
  18.0 2.5 %shard_map.63 = (bf16[128,8,256]{2,1,0:T(8,128)(2,1)S(1)}, bf16[128,8,256]{2,1,0:T(8,128)(2,1)S(1)}, bf16[128,8,256]{2,1,0:T(8,128)(2,1)S(1)}, bf16[128,8,256]{2,1,0:T(8,128)(2,1)S(1)}) custom-call(s32[4]{0:T(128)S(1)} %pad_add_fusion.1.here_ref, s32[512]{0:T(512)S(1)} %copy-done.1, bf16[16,256,256]{2,1,0:T(8,128)(2,1)S(1)} %get-tuple-element.41.weights, ...), custom_call_target="tpu_custom_call" | custom-call | flops 256000000 | bytes 1048576 | tf_op jit(solution)/shard_map/pallas_call | solution.py:264
  22.3 2.5 %shard_map.64 = (bf16[128,8,256]{2,1,0:T(8,128)(2,1)S(1)}, bf16[128,8,256]{2,1,0:T(8,128)(2,1)S(1)}, bf16[128,8,256]{2,1,0:T(8,128)(2,1)S(1)}, bf16[128,8,256]{2,1,0:T(8,128)(2,1)S(1)}) custom-call(s32[4]{0:T(128)S(1)} %pad_add_fusion.1.here_ref, s32[512]{0:T(512)S(1)} %copy-done.1, bf16[16,256,256]{2,1,0:T(8,128)(2,1)S(1)} %get-tuple-element.41.weights, ...), custom_call_target="tpu_custom_call" | custom-call | flops 256000000 | bytes 1048576 | tf_op jit(solution)/shard_map/pallas_call | solution.py:264
  24.8 6.0 %collective-permute-done.3.b_ref = bf16[128,8,512]{2,1,0:T(8,128)(2,1)S(1)} collective-permute-done((bf16[128,8,512]{2,1,0:T(8,128)(2,1)S(1)}, bf16[128,8,512]{2,1,0:T(8,128)(2,1)S(1)}, u32[]{:S(2)}, u32[]{:S(2)}) %collective-permute-start.3) | collective-permute-done | bytes 1048608 | tf_op jit(solution)/shard_map/ppermute | solution.py:48
  33.0 3.8 %collective-permute-done.8.b_ref = bf16[128,8,256]{2,1,0:T(8,128)(2,1)S(1)} collective-permute-done((bf16[128,8,256]{2,1,0:T(8,128)(2,1)S(1)}, bf16[128,8,256]{2,1,0:T(8,128)(2,1)S(1)}, u32[]{:S(2)}, u32[]{:S(2)}) %collective-permute-start.8) | collective-permute-done | bytes 524320 | tf_op jit(solution)/shard_map/ppermute | solution.py:48
  36.9 2.9 %collective-permute-start.9 = (bf16[128,8,256]{2,1,0:T(8,128)(2,1)S(1)}, bf16[128,8,256]{2,1,0:T(8,128)(2,1)S(1)}, u32[]{:S(2)}, u32[]{:S(2)}) collective-permute-start(bf16[128,8,256]{2,1,0:T(8,128)(2,1)S(1)} %shard_map.66), channel_id=1, source_target_pairs={{0,96},{1,97},{2,26},{3,27},{4,100},{5,101},{6,30},{7,31},{8,104},... | collective-permute-start | bytes 1572872 | tf_op jit(solution)/shard_map/ppermute | solution.py:48
  39.9 4.0 %collective-permute-start.13 = (bf16[128,8,256]{2,1,0:T(8,128)(2,1)S(1)}, bf16[128,8,256]{2,1,0:T(8,128)(2,1)S(1)}, u32[]{:S(2)}, u32[]{:S(2)}) collective-permute-start(bf16[128,8,256]{2,1,0:T(8,128)(2,1)S(1)} %get-tuple-element.58), channel_id=1, source_target_pairs={{0,1},{1,0},{2,3},{3,2},{4,5},{5,4},{6,7},{7,6},{8,9},{9,8},{10,11... | collective-permute-start | bytes 1572872 | tf_op jit(solution)/shard_map/ppermute | solution.py:48
  43.8 8.9 %collective-permute-done.7.refs_4_ = bf16[128,8,256]{2,1,0:T(8,128)(2,1)S(1)} collective-permute-done((bf16[128,8,256]{2,1,0:T(8,128)(2,1)S(1)}, bf16[128,8,256]{2,1,0:T(8,128)(2,1)S(1)}, u32[]{:S(2)}, u32[]{:S(2)}) %collective-permute-start.7) | collective-permute-done | bytes 524320 | tf_op jit(solution)/shard_map/ppermute | solution.py:48
  52.7 2.0 %collective-permute-start.14 = (bf16[128,8,256]{2,1,0:T(8,128)(2,1)S(1)}, bf16[128,8,256]{2,1,0:T(8,128)(2,1)S(1)}, u32[]{:S(2)}, u32[]{:S(2)}) collective-permute-start(bf16[128,8,256]{2,1,0:T(8,128)(2,1)S(1)} %get-tuple-element.59), channel_id=1, source_target_pairs={{0,4},{1,5},{2,6},{3,7},{4,1},{5,0},{6,3},{7,2},{8,12},{9,13},{10,... | collective-permute-start | bytes 1572872 | tf_op jit(solution)/shard_map/ppermute | solution.py:48
  54.8 2.1 %collective-permute-start.15 = (bf16[128,8,256]{2,1,0:T(8,128)(2,1)S(1)}, bf16[128,8,256]{2,1,0:T(8,128)(2,1)S(1)}, u32[]{:S(2)}, u32[]{:S(2)}) collective-permute-start(bf16[128,8,256]{2,1,0:T(8,128)(2,1)S(1)} %get-tuple-element.60), channel_id=1, source_target_pairs={{0,5},{1,4},{2,7},{3,6},{4,0},{5,1},{6,2},{7,3},{8,13},{9,12},{10,... | collective-permute-start | bytes 1572872 | tf_op jit(solution)/shard_map/ppermute | solution.py:48
  57.9 3.2 %collective-permute-start.10 = (bf16[32,8,768]{2,1,0:T(8,128)(2,1)S(1)}, bf16[32,8,768]{2,1,0:T(8,128)(2,1)S(1)}, u32[]{:S(2)}, u32[]{:S(2)}) collective-permute-start(bf16[32,8,768]{2,1,0:T(8,128)(2,1)S(1)} %get-tuple-element.55), channel_id=1, source_target_pairs={{0,16},{1,17},{2,3},{3,2},{4,20},{5,21},{6,7},{7,6},{8,24},{9,25},... | collective-permute-start | bytes 1179656 | tf_op jit(solution)/shard_map/ppermute | solution.py:48
  61.8 2.6 %collective-permute-start.12 = (bf16[32,8,768]{2,1,0:T(8,128)(2,1)S(1)}, bf16[32,8,768]{2,1,0:T(8,128)(2,1)S(1)}, u32[]{:S(2)}, u32[]{:S(2)}) collective-permute-start(bf16[32,8,768]{2,1,0:T(8,128)(2,1)S(1)} %get-tuple-element.57), channel_id=1, source_target_pairs={{0,24},{1,25},{2,7},{3,6},{4,28},{5,29},{6,2},{7,3},{8,0},{9,1},{1... | collective-permute-start | bytes 1179656 | tf_op jit(solution)/shard_map/ppermute | solution.py:48
  64.4 9.5 %collective-permute-done.14.refs_2_ = bf16[128,8,256]{2,1,0:T(8,128)(2,1)S(1)} collective-permute-done((bf16[128,8,256]{2,1,0:T(8,128)(2,1)S(1)}, bf16[128,8,256]{2,1,0:T(8,128)(2,1)S(1)}, u32[]{:S(2)}, u32[]{:S(2)}) %collective-permute-start.14) | collective-permute-done | bytes 524320 | tf_op jit(solution)/shard_map/ppermute | solution.py:48
  75.4 2.5 %collective-permute-start.21 = (bf16[32,8,256]{2,1,0:T(8,128)(2,1)S(1)}, bf16[32,8,256]{2,1,0:T(8,128)(2,1)S(1)}, u32[]{:S(2)}, u32[]{:S(2)}) collective-permute-start(bf16[32,8,256]{2,1,0:T(8,128)(2,1)S(1)} %get-tuple-element.68), channel_id=1, source_target_pairs={{0,96},{1,97},{2,98},{3,99},{4,100},{5,101},{6,102},{7,103},{8,104... | collective-permute-start | bytes 393224 | tf_op jit(solution)/shard_map/ppermute | solution.py:48
  78.1 3.4 %collective-permute-done.19.refs_1_ = bf16[32,8,256]{2,1,0:T(8,128)(2,1)S(1)} collective-permute-done((bf16[32,8,256]{2,1,0:T(8,128)(2,1)}, bf16[32,8,256]{2,1,0:T(8,128)(2,1)S(1)}, u32[]{:S(2)}, u32[]{:S(2)}) %collective-permute-start.19) | collective-permute-done | bytes 131104 | tf_op jit(solution)/shard_map/ppermute | solution.py:48
  82.3 3.3 %collective-permute-start.22 = (bf16[8,8,256]{2,1,0:T(8,128)(2,1)S(1)}, bf16[8,8,256]{2,1,0:T(8,128)(2,1)S(1)}, u32[]{:S(2)}, u32[]{:S(2)}) collective-permute-start(bf16[8,8,256]{2,1,0:T(8,128)(2,1)S(1)} %get-tuple-element.70), channel_id=1, source_target_pairs={{0,16},{1,17},{2,18},{3,19},{4,20},{5,21},{6,22},{7,23},{8,24},{9,... | collective-permute-start | bytes 98312 | tf_op jit(solution)/shard_map/ppermute | solution.py:48
  85.7 2.9 %collective-permute-start.16 = (bf16[8,8,768]{2,1,0:T(8,128)(2,1)S(1)}, bf16[8,8,768]{2,1,0:T(8,128)(2,1)S(1)}, u32[]{:S(2)}, u32[]{:S(2)}) collective-permute-start(bf16[8,8,768]{2,1,0:T(8,128)(2,1)S(1)} %get-tuple-element.63), channel_id=1, source_target_pairs={{0,1},{1,0},{2,66},{3,67},{4,5},{5,4},{6,70},{7,71},{8,9},{9,8},{1... | collective-permute-start | bytes 294920 | tf_op jit(solution)/shard_map/ppermute | solution.py:48
  89.5 2.3 %collective-permute-start.18 = (bf16[8,8,768]{2,1,0:T(8,128)(2,1)S(1)}, bf16[8,8,768]{2,1,0:T(8,128)(2,1)S(1)}, u32[]{:S(2)}, u32[]{:S(2)}) collective-permute-start(bf16[8,8,768]{2,1,0:T(8,128)(2,1)S(1)} %get-tuple-element.65), channel_id=1, source_target_pairs={{0,5},{1,4},{2,98},{3,99},{4,0},{5,1},{6,102},{7,103},{8,13},{9,12... | collective-permute-start | bytes 294920 | tf_op jit(solution)/shard_map/ppermute | solution.py:48
  91.8 1.8 %collective-permute-start.23 = (bf16[8,8,256]{2,1,0:T(8,128)(2,1)S(1)}, bf16[8,8,256]{2,1,0:T(8,128)(2,1)S(1)}, u32[]{:S(2)}, u32[]{:S(2)}) collective-permute-start(bf16[8,8,256]{2,1,0:T(8,128)(2,1)S(1)} %get-tuple-element.71), channel_id=1, source_target_pairs={{0,8},{1,9},{2,10},{3,11},{4,12},{5,13},{6,14},{7,15},{8,16},{9,17... | collective-permute-start | bytes 98312 | tf_op jit(solution)/shard_map/ppermute | solution.py:48
  99.6 7.5 %all-to-all-start = ((f32[128,1,160]{2,1,0:T(1,128)}), f32[128,1,160]{2,1,0:T(1,128)S(1)}, u32[]{:S(2)}, u32[]{:S(2)}) async-start(f32[128,1,160]{2,1,0:T(1,128)} %copy.8), calls=%async_computation | async-start | bytes 262144 | tf_op jit(solution)/shard_map/all_to_all | solution.py:428
  107.2 9.1 %all-to-all-done = f32[128,1,160]{2,1,0:T(1,128)S(1)} async-done(((f32[128,1,160]{2,1,0:T(1,128)}), f32[128,1,160]{2,1,0:T(1,128)S(1)}, u32[]{:S(2)}, u32[]{:S(2)}) %all-to-all-start) | async-done | bytes 81952 | tf_op jit(solution)/shard_map/all_to_all | solution.py:428
  (60 shorter events, 22.8 us)
Async XLA Ops:
  5.0 7.4 %collective-permute-start.1 = (bf16[4,512,512]{2,1,0:T(8,128)(2,1)}, bf16[4,512,512]{2,1,0:T(8,128)(2,1)S(1)}, u32[]{:S(2)}, u32[]{:S(2)}) collective-permute-start(bf16[4,512,512]{2,1,0:T(8,128)(2,1)} %get-tuple-element.43), channel_id=1, source_target_pairs={{0,2},{2,0},{1,3},{3,1},{4,6},{6,4},{5,7},{7,5},{8,10},{10,8},{9,1... | collective-permute-start | bytes 6291464 | tf_op jit(solution)/shard_map/ppermute | solution.py:52
  5.6 16.7 %collective-permute-start.4 = (bf16[4,512,256]{2,1,0:T(8,128)(2,1)}, bf16[4,512,256]{2,1,0:T(8,128)(2,1)}, u32[]{:S(2)}, u32[]{:S(2)}) collective-permute-start(bf16[4,512,256]{2,1,0:T(8,128)(2,1)} %get-tuple-element.48), channel_id=1, source_target_pairs={{0,2},{2,0},{1,3},{3,1},{4,6},{6,4},{5,7},{7,5},{8,10},{10,8},{9,1... | collective-permute-start | bytes 3145736 | tf_op jit(solution)/shard_map/ppermute | solution.py:52
  6.9 11.1 %collective-permute-start.5 = (bf16[4,512,256]{2,1,0:T(8,128)(2,1)S(1)}, bf16[4,512,256]{2,1,0:T(8,128)(2,1)}, u32[]{:S(2)}, u32[]{:S(2)}) collective-permute-start(bf16[4,512,256]{2,1,0:T(8,128)(2,1)S(1)} %shard_map.60.rest_0_), channel_id=1, source_target_pairs={{0,2},{2,0},{1,3},{3,1},{4,6},{6,4},{5,7},{7,5},{8,10},{10,8},{9,1... | collective-permute-start | bytes 3145736 | tf_op jit(solution)/shard_map/ppermute | solution.py:52
  14.7 16.1 %collective-permute-start.3 = (bf16[128,8,512]{2,1,0:T(8,128)(2,1)S(1)}, bf16[128,8,512]{2,1,0:T(8,128)(2,1)S(1)}, u32[]{:S(2)}, u32[]{:S(2)}) collective-permute-start(bf16[128,8,512]{2,1,0:T(8,128)(2,1)S(1)} %get-tuple-element.47), channel_id=1, source_target_pairs={{0,32},{1,33},{2,10},{3,11},{4,36},{5,37},{6,14},{7,15},{8,40},{9,... | collective-permute-start | bytes 3145736 | tf_op jit(solution)/shard_map/ppermute | solution.py:48
  16.4 38.4 %collective-permute-start.2 = (bf16[128,8,512]{2,1,0:T(8,128)(2,1)S(1)}, bf16[128,8,512]{2,1,0:T(8,128)(2,1)S(1)}, u32[]{:S(2)}, u32[]{:S(2)}) collective-permute-start(bf16[128,8,512]{2,1,0:T(8,128)(2,1)S(1)} %get-tuple-element.45), channel_id=1, source_target_pairs={{0,96},{1,97},{2,26},{3,27},{4,100},{5,101},{6,30},{7,31},{8,104},... | collective-permute-start | bytes 3145736 | tf_op jit(solution)/shard_map/ppermute | solution.py:48
  20.5 16.3 %collective-permute-start.8 = (bf16[128,8,256]{2,1,0:T(8,128)(2,1)S(1)}, bf16[128,8,256]{2,1,0:T(8,128)(2,1)S(1)}, u32[]{:S(2)}, u32[]{:S(2)}) collective-permute-start(bf16[128,8,256]{2,1,0:T(8,128)(2,1)S(1)} %get-tuple-element.53), channel_id=1, source_target_pairs={{0,96},{1,97},{2,26},{3,27},{4,100},{5,101},{6,30},{7,31},{8,104},... | collective-permute-start | bytes 1572872 | tf_op jit(solution)/shard_map/ppermute | solution.py:48
  31.0 25.9 %collective-permute-start.6 = (bf16[128,8,512]{2,1,0:T(8,128)(2,1)S(1)}, bf16[128,8,512]{2,1,0:T(8,128)(2,1)S(1)}, u32[]{:S(2)}, u32[]{:S(2)}) collective-permute-start(bf16[128,8,512]{2,1,0:T(8,128)(2,1)S(1)} %shard_map.65.rest_0_), channel_id=1, source_target_pairs={{0,32},{1,33},{2,10},{3,11},{4,36},{5,37},{6,14},{7,15},{8,40},{9,... | collective-permute-start | bytes 3145736 | tf_op jit(solution)/shard_map/ppermute | solution.py:48
  31.5 21.2 %collective-permute-start.7 = (bf16[128,8,256]{2,1,0:T(8,128)(2,1)S(1)}, bf16[128,8,256]{2,1,0:T(8,128)(2,1)S(1)}, u32[]{:S(2)}, u32[]{:S(2)}) collective-permute-start(bf16[128,8,256]{2,1,0:T(8,128)(2,1)S(1)} %get-tuple-element.51), channel_id=1, source_target_pairs={{0,32},{1,33},{2,10},{3,11},{4,36},{5,37},{6,14},{7,15},{8,40},{9,... | collective-permute-start | bytes 1572872 | tf_op jit(solution)/shard_map/ppermute | solution.py:48
  36.9 20.0 %collective-permute-start.9 = (bf16[128,8,256]{2,1,0:T(8,128)(2,1)S(1)}, bf16[128,8,256]{2,1,0:T(8,128)(2,1)S(1)}, u32[]{:S(2)}, u32[]{:S(2)}) collective-permute-start(bf16[128,8,256]{2,1,0:T(8,128)(2,1)S(1)} %shard_map.66), channel_id=1, source_target_pairs={{0,96},{1,97},{2,26},{3,27},{4,100},{5,101},{6,30},{7,31},{8,104},... | collective-permute-start | bytes 1572872 | tf_op jit(solution)/shard_map/ppermute | solution.py:48
  39.9 22.0 %collective-permute-start.13 = (bf16[128,8,256]{2,1,0:T(8,128)(2,1)S(1)}, bf16[128,8,256]{2,1,0:T(8,128)(2,1)S(1)}, u32[]{:S(2)}, u32[]{:S(2)}) collective-permute-start(bf16[128,8,256]{2,1,0:T(8,128)(2,1)S(1)} %get-tuple-element.58), channel_id=1, source_target_pairs={{0,1},{1,0},{2,3},{3,2},{4,5},{5,4},{6,7},{7,6},{8,9},{9,8},{10,11... | collective-permute-start | bytes 1572872 | tf_op jit(solution)/shard_map/ppermute | solution.py:48
  52.7 21.1 %collective-permute-start.14 = (bf16[128,8,256]{2,1,0:T(8,128)(2,1)S(1)}, bf16[128,8,256]{2,1,0:T(8,128)(2,1)S(1)}, u32[]{:S(2)}, u32[]{:S(2)}) collective-permute-start(bf16[128,8,256]{2,1,0:T(8,128)(2,1)S(1)} %get-tuple-element.59), channel_id=1, source_target_pairs={{0,4},{1,5},{2,6},{3,7},{4,1},{5,0},{6,3},{7,2},{8,12},{9,13},{10,... | collective-permute-start | bytes 1572872 | tf_op jit(solution)/shard_map/ppermute | solution.py:48
  54.8 19.1 %collective-permute-start.15 = (bf16[128,8,256]{2,1,0:T(8,128)(2,1)S(1)}, bf16[128,8,256]{2,1,0:T(8,128)(2,1)S(1)}, u32[]{:S(2)}, u32[]{:S(2)}) collective-permute-start(bf16[128,8,256]{2,1,0:T(8,128)(2,1)S(1)} %get-tuple-element.60), channel_id=1, source_target_pairs={{0,5},{1,4},{2,7},{3,6},{4,0},{5,1},{6,2},{7,3},{8,13},{9,12},{10,... | collective-permute-start | bytes 1572872 | tf_op jit(solution)/shard_map/ppermute | solution.py:48
  57.9 17.4 %collective-permute-start.10 = (bf16[32,8,768]{2,1,0:T(8,128)(2,1)S(1)}, bf16[32,8,768]{2,1,0:T(8,128)(2,1)S(1)}, u32[]{:S(2)}, u32[]{:S(2)}) collective-permute-start(bf16[32,8,768]{2,1,0:T(8,128)(2,1)S(1)} %get-tuple-element.55), channel_id=1, source_target_pairs={{0,16},{1,17},{2,3},{3,2},{4,20},{5,21},{6,7},{7,6},{8,24},{9,25},... | collective-permute-start | bytes 1179656 | tf_op jit(solution)/shard_map/ppermute | solution.py:48
  61.1 16.8 %collective-permute-start.11 = (bf16[32,8,768]{2,1,0:T(8,128)(2,1)}, bf16[32,8,768]{2,1,0:T(8,128)(2,1)S(1)}, u32[]{:S(2)}, u32[]{:S(2)}) collective-permute-start(bf16[32,8,768]{2,1,0:T(8,128)(2,1)} %get-tuple-element.56), channel_id=1, source_target_pairs={{0,8},{1,9},{2,6},{3,7},{4,12},{5,13},{6,3},{7,2},{8,16},{9,17},{1... | collective-permute-start | bytes 1179656 | tf_op jit(solution)/shard_map/ppermute | solution.py:48
  61.8 16.1 %collective-permute-start.12 = (bf16[32,8,768]{2,1,0:T(8,128)(2,1)S(1)}, bf16[32,8,768]{2,1,0:T(8,128)(2,1)S(1)}, u32[]{:S(2)}, u32[]{:S(2)}) collective-permute-start(bf16[32,8,768]{2,1,0:T(8,128)(2,1)S(1)} %get-tuple-element.57), channel_id=1, source_target_pairs={{0,24},{1,25},{2,7},{3,6},{4,28},{5,29},{6,2},{7,3},{8,0},{9,1},{1... | collective-permute-start | bytes 1179656 | tf_op jit(solution)/shard_map/ppermute | solution.py:48
  74.7 6.8 %collective-permute-start.19 = (bf16[32,8,256]{2,1,0:T(8,128)(2,1)}, bf16[32,8,256]{2,1,0:T(8,128)(2,1)S(1)}, u32[]{:S(2)}, u32[]{:S(2)}) collective-permute-start(bf16[32,8,256]{2,1,0:T(8,128)(2,1)} %get-tuple-element.66), channel_id=1, source_target_pairs={{0,64},{1,65},{2,66},{3,67},{4,68},{5,69},{6,70},{7,71},{8,72},{9,... | collective-permute-start | bytes 393224 | tf_op jit(solution)/shard_map/ppermute | solution.py:48
  74.7 7.6 %collective-permute-start.20 = (bf16[32,8,256]{2,1,0:T(8,128)(2,1)S(1)}, bf16[32,8,256]{2,1,0:T(8,128)(2,1)S(1)}, u32[]{:S(2)}, u32[]{:S(2)}) collective-permute-start(bf16[32,8,256]{2,1,0:T(8,128)(2,1)S(1)} %get-tuple-element.67), channel_id=1, source_target_pairs={{0,32},{1,33},{2,34},{3,35},{4,36},{5,37},{6,38},{7,39},{8,40},{9,... | collective-permute-start | bytes 393224 | tf_op jit(solution)/shard_map/ppermute | solution.py:48
  75.4 6.9 %collective-permute-start.21 = (bf16[32,8,256]{2,1,0:T(8,128)(2,1)S(1)}, bf16[32,8,256]{2,1,0:T(8,128)(2,1)S(1)}, u32[]{:S(2)}, u32[]{:S(2)}) collective-permute-start(bf16[32,8,256]{2,1,0:T(8,128)(2,1)S(1)} %get-tuple-element.68), channel_id=1, source_target_pairs={{0,96},{1,97},{2,98},{3,99},{4,100},{5,101},{6,102},{7,103},{8,104... | collective-permute-start | bytes 393224 | tf_op jit(solution)/shard_map/ppermute | solution.py:48
  82.3 11.4 %collective-permute-start.22 = (bf16[8,8,256]{2,1,0:T(8,128)(2,1)S(1)}, bf16[8,8,256]{2,1,0:T(8,128)(2,1)S(1)}, u32[]{:S(2)}, u32[]{:S(2)}) collective-permute-start(bf16[8,8,256]{2,1,0:T(8,128)(2,1)S(1)} %get-tuple-element.70), channel_id=1, source_target_pairs={{0,16},{1,17},{2,18},{3,19},{4,20},{5,21},{6,22},{7,23},{8,24},{9,... | collective-permute-start | bytes 98312 | tf_op jit(solution)/shard_map/ppermute | solution.py:48
  85.7 11.9 %collective-permute-start.16 = (bf16[8,8,768]{2,1,0:T(8,128)(2,1)S(1)}, bf16[8,8,768]{2,1,0:T(8,128)(2,1)S(1)}, u32[]{:S(2)}, u32[]{:S(2)}) collective-permute-start(bf16[8,8,768]{2,1,0:T(8,128)(2,1)S(1)} %get-tuple-element.63), channel_id=1, source_target_pairs={{0,1},{1,0},{2,66},{3,67},{4,5},{5,4},{6,70},{7,71},{8,9},{9,8},{1... | collective-permute-start | bytes 294920 | tf_op jit(solution)/shard_map/ppermute | solution.py:48
  88.6 9.0 %collective-permute-start.17 = (bf16[8,8,768]{2,1,0:T(8,128)(2,1)S(1)}, bf16[8,8,768]{2,1,0:T(8,128)(2,1)S(1)}, u32[]{:S(2)}, u32[]{:S(2)}) collective-permute-start(bf16[8,8,768]{2,1,0:T(8,128)(2,1)S(1)} %get-tuple-element.64), channel_id=1, source_target_pairs={{0,4},{1,5},{2,34},{3,35},{4,1},{5,0},{6,38},{7,39},{8,12},{9,13},... | collective-permute-start | bytes 294920 | tf_op jit(solution)/shard_map/ppermute | solution.py:48
  89.5 8.1 %collective-permute-start.18 = (bf16[8,8,768]{2,1,0:T(8,128)(2,1)S(1)}, bf16[8,8,768]{2,1,0:T(8,128)(2,1)S(1)}, u32[]{:S(2)}, u32[]{:S(2)}) collective-permute-start(bf16[8,8,768]{2,1,0:T(8,128)(2,1)S(1)} %get-tuple-element.65), channel_id=1, source_target_pairs={{0,5},{1,4},{2,98},{3,99},{4,0},{5,1},{6,102},{7,103},{8,13},{9,12... | collective-permute-start | bytes 294920 | tf_op jit(solution)/shard_map/ppermute | solution.py:48
  99.6 16.8 %all-to-all-start = ((f32[128,1,160]{2,1,0:T(1,128)}), f32[128,1,160]{2,1,0:T(1,128)S(1)}, u32[]{:S(2)}, u32[]{:S(2)}) async-start(f32[128,1,160]{2,1,0:T(1,128)} %copy.8), calls=%async_computation | async-start | bytes 262144 | tf_op jit(solution)/shard_map/all_to_all | solution.py:428
  107.1 10.1 %collective-permute-start.25 = (f32[4,8,1024]{2,1,0:T(8,128)S(1)}, f32[4,8,1024]{2,1,0:T(8,128)S(1)}, u32[]{:S(2)}, u32[]{:S(2)}) collective-permute-start(f32[4,8,1024]{2,1,0:T(8,128)S(1)} %get-tuple-element.74), channel_id=1, source_target_pairs={{0,2},{2,0},{1,3},{3,1},{4,6},{6,4},{5,7},{7,5},{8,10},{10,8},{9,1... | collective-permute-start | bytes 393224 | tf_op jit(solution)/shard_map/ppermute | solution.py:52
  (5 other events, 20.3 us)

commit v3 on v2

--- a/solution.py
+++ b/solution.py
@@ -18,7 +18,7 @@
     (768, 256, ((Z, X, Y), (Z, X, Y))),
 )
 PIECES = ((0, 512, 0), (512, 256, 0), (768, 256, 1))
-SHIFTS = (2, 1, 3)
+SHIFTS = (1, 3, 2)
 F32, BF16 = jnp.float32, jnp.bfloat16
 SMEM = pl.BlockSpec(memory_space=pltpu.SMEM)
 VMEM = pl.BlockSpec(memory_space=pltpu.VMEM)
@@ -61,13 +61,30 @@
     )
 
 
-def half_copy(first, width, core_ref, leg_ref, out_ref, sem):
+class Copies:
+    def __init__(self, sources, sems, base=0):
+        self.copies = [pltpu.make_async_copy(a, b, sems.at[base + k]) for k, (a, b) in enumerate(sources)]
+
+    def start(self):
+        for copy in self.copies:
+            copy.start()
+
+    def wait(self):
+        for copy in self.copies:
+            copy.wait()
+
+
+def columns_copy(start, width, leg_ref, out_ref, sems, base=0):
+    return Copies([(leg_ref.at[r, :, pl.ds(start, width)], out_ref.at[r]) for r in range(4)], sems, base)
+
+
+def half_copy(first, width, core_ref, leg_ref, out_ref, sems, base=0):
     start = pl.multiple_of((1 - core_ref[0]) * 1024 + first, 128)
-    return pltpu.make_async_copy(leg_ref.at[:, :, pl.ds(start, width)], out_ref, sem)
-
-
-def half_kernel(core_ref, leg_ref, out_ref, sem):
-    copy = half_copy(*PIECES[1][:2], core_ref, leg_ref, out_ref, sem)
+    return columns_copy(start, width, leg_ref, out_ref, sems, base)
+
+
+def half_kernel(core_ref, leg_ref, out_ref, sems):
+    copy = half_copy(*PIECES[1][:2], core_ref, leg_ref, out_ref, sems)
     copy.start()
     copy.wait()
 
@@ -80,7 +97,7 @@
         out_shape=jax.ShapeDtypeStruct((4, 512, PIECES[1][1]), BF16),
         in_specs=[SMEM, HBM],
         out_specs=VMEM,
-        scratch_shapes=[pltpu.SemaphoreType.DMA],
+        scratch_shapes=[pltpu.SemaphoreType.DMA((4,))],
     )(core, legendre)
 
 
@@ -124,13 +141,13 @@
 def fourier_kernel(
     core_ref, leg_ref, sky_ref, waves_ref, out_ref, send_ref, half_ref, last_ref, x_ref, cos_ref, sin_ref, tail_ref, z_ref, sems
 ):
-    half = half_copy(*PIECES[0][:2], core_ref, leg_ref, half_ref, sems.at[0])
-    last = half_copy(*PIECES[2][:2], core_ref, leg_ref, last_ref, sems.at[5])
+    half = half_copy(*PIECES[0][:2], core_ref, leg_ref, half_ref, sems, 0)
+    last = half_copy(*PIECES[2][:2], core_ref, leg_ref, last_ref, sems, 4)
     copies = [
-        pltpu.make_async_copy(sky_ref, x_ref, sems.at[1]),
-        pltpu.make_async_copy(waves_ref.at[0:32], cos_ref, sems.at[2]),
-        pltpu.make_async_copy(waves_ref.at[32:64], sin_ref, sems.at[3]),
-        pltpu.make_async_copy(waves_ref.at[64:320], tail_ref, sems.at[4]),
+        pltpu.make_async_copy(sky_ref, x_ref, sems.at[8]),
+        pltpu.make_async_copy(waves_ref.at[0:32], cos_ref, sems.at[9]),
+        pltpu.make_async_copy(waves_ref.at[32:64], sin_ref, sems.at[10]),
+        pltpu.make_async_copy(waves_ref.at[64:320], tail_ref, sems.at[11]),
     ]
     for copy in copies:
         copy.start()
@@ -187,15 +204,15 @@
             pltpu.VMEM((32, 128), F32),
             pltpu.VMEM((256, 128), F32),
             pltpu.VMEM((256, 256), F32),
-            pltpu.SemaphoreType.DMA((6,)),
+            pltpu.SemaphoreType.DMA((12,)),
         ],
     )(core, legendre, sky_maps, jnp.asarray(waves, F32))
 
 
 def weights_kernel(core_ref, leg_ref, own_ref, got_ref, *rest):
-    out_ref, table_ref, sem = rest[-3:]
+    out_ref, table_ref, sems = rest[-3:]
     start = pl.multiple_of(core_ref[0] * 1024, 128)
-    copy = pltpu.make_async_copy(leg_ref.at[:, :, pl.ds(start, 1024)], table_ref, sem)
+    copy = columns_copy(start, 1024, leg_ref, table_ref, sems)
     copy.start()
     order_weights(own_ref, got_ref, out_ref)
     copy.wait()
@@ -209,7 +226,7 @@
         out_shape=[jax.ShapeDtypeStruct((16, 256, 256), BF16), jax.ShapeDtypeStruct((4, 512, 1024), BF16)],
         in_specs=[SMEM, HBM, VMEM, VMEM] + [HBM] * len(after),
         out_specs=[VMEM] * 2,
-        scratch_shapes=[pltpu.SemaphoreType.DMA],
+        scratch_shapes=[pltpu.SemaphoreType.DMA((4,))],
     )(core, legendre, own_f, got_f, *after)
 
 
@@ -391,7 +408,7 @@
         return shift_along(block, (axes[0][stage], axes[1][stage]), shift)
 
     def exchange(sent, stage, colour):
-        return [sent[0]] + [move(sent[d], stage, colour, d) for d in SHIFTS]
+        return [sent[0]] + [move(sent[d], stage, colour, d) for d in (SHIFTS if stage == 2 else (2, 1, 3))]
 
     def sums_of(k, got, *after):
         return chip_sums(PIECES[k], here_scalars, owner_table, weights, table, got, *after)

time: 119 us -> 119 us (level)
    ppermute x21, starting transfers between devices: 40.4 us -> 38.9 us  [shift_along(): return lax.ppermute(x, BLK_GRP, pairs)]
  transfers between devices with their start and end apart: 27 -> 27, of which waited for: 10 -> 9; matrix products, arithmetic and copies ran while one was open for 1% -> 1% of each run, Pallas kernels for 12% -> 11%
where the time goes in v3:
time: 119 us; the launch traced here: 118 us
  starting transfers between devices  48.8 us (41%)
  waiting for transfers between devices  46.5 us (39%)
  Pallas kernels  18.3 us (15%)
  local copies, waits for them, and re-layouts  2.21 us (2%)
    ppermute x21, starting transfers between devices, shift_along(): return lax.ppermute(x, BLK_GRP, pairs)  38.9 us
    ppermute x21, waiting for transfers between devices, shift_along(): return lax.ppermute(x, BLK_GRP, pairs)  35.3 us
    all_to_all x1, waiting for transfers between devices, steps(): power = lax.all_to_all(terms, BLK_GRP, 0, 0, tiled=True)  9.12 us
    all_to_all x1, starting transfers between devices, steps(): power = lax.all_to_all(terms, BLK_GRP, 0, 0, tiled=True)  8.56 us
    pallas_call x3, Pallas kernels, chip_sums(): kernel_call(functools.partial(chip_sums_kernel, first, width, COLOURS[col...  7.38 us
    pallas_call x1, Pallas kernels, fourier_and_half(): kernel_call(fourier_kernel, 55, 1 << 22, out_shape=[jax.ShapeDtypeStruct(...  4.36 us
  transfers between devices with their start and end apart: 27, of which 9 were waited for; matrix products, arithmetic and copies ran while one was open for 1% of the time, Pallas kernels for 11%

profile of v3, /device:TPU:0, one launch (start us, length us, event | category | flops | bytes accessed | tf_op | source)
XLA Modules:
  0.0 117.6 jit_solution(8403202044153295230)
XLA Ops:
  0.7 4.4 %shard_map.59 = (bf16[256,128]{1,0:T(8,128)(2,1)}, bf16[256,128]{1,0:T(8,128)(2,1)}, bf16[4,512,512]{2,1,0:T(8,128)(2,1)}, bf16[4,512,256]{2,1,0:T(8,128)(2,1)}) custom-call(s32[1]{0:T(128)} %bitcast.core_ref, bf16[4,512,2048]{2,1,0:T(8,128)(2,1)} %leg_ref.5, f32[4,4,4096]{2,1,0:T(4,128)} %sky_ref.1, f32[320,128]{1,0:T(8,128)} %constant.115.clone.waves_ref), custom_call_target="tpu_custom_call" | custom-call | flops 4194304 | bytes 1048576 | tf_op jit(solution)/shard_map/pallas_call | solution.py:193
  7.5 2.0 %collective-permute-done.got_ref = bf16[256,128]{1,0:T(8,128)(2,1)S(1)} collective-permute-done((bf16[256,128]{1,0:T(8,128)(2,1)}, bf16[256,128]{1,0:T(8,128)(2,1)S(1)}, u32[]{:S(2)}, u32[]{:S(2)}) %collective-permute-start) | collective-permute-done | bytes 65568 | tf_op jit(solution)/shard_map/ppermute | solution.py:52
  9.6 2.2 %shard_map.61 = (bf16[16,256,256]{2,1,0:T(8,128)(2,1)S(1)}, bf16[4,512,1024]{2,1,0:T(8,128)(2,1)S(1)}) custom-call(s32[1]{0:T(128)} %bitcast.core_ref, bf16[4,512,2048]{2,1,0:T(8,128)(2,1)} %leg_ref.5, bf16[256,128]{1,0:T(8,128)(2,1)S(1)} %copy-done, bf16[256,128]{1,0:T(8,128)(2,1)S(1)} %collective-permute-done.got_ref, ...), custom_call_target="tpu_custom_call" | custom-call | flops 67108864 | bytes 1048576 | tf_op jit(solution)/shard_map/pallas_call | solution.py:222
  11.8 2.4 %shard_map.62 = (bf16[128,8,512]{2,1,0:T(8,128)(2,1)S(1)}, bf16[128,8,512]{2,1,0:T(8,128)(2,1)S(1)}, bf16[128,8,512]{2,1,0:T(8,128)(2,1)S(1)}, bf16[128,8,512]{2,1,0:T(8,128)(2,1)S(1)}) custom-call(s32[4]{0:T(128)S(1)} %pad_add_fusion.1.here_ref, s32[512]{0:T(512)S(1)} %copy-done.1, bf16[16,256,256]{2,1,0:T(8,128)(2,1)S(1)} %get-tuple-element.41.weights, ...), custom_call_target="tpu_custom_call" | custom-call | flops 512000000 | bytes 1048576 | tf_op jit(solution)/shard_map/pallas_call | solution.py:281
  17.5 2.5 %shard_map.63 = (bf16[128,8,256]{2,1,0:T(8,128)(2,1)S(1)}, bf16[128,8,256]{2,1,0:T(8,128)(2,1)S(1)}, bf16[128,8,256]{2,1,0:T(8,128)(2,1)S(1)}, bf16[128,8,256]{2,1,0:T(8,128)(2,1)S(1)}) custom-call(s32[4]{0:T(128)S(1)} %pad_add_fusion.1.here_ref, s32[512]{0:T(512)S(1)} %copy-done.1, bf16[16,256,256]{2,1,0:T(8,128)(2,1)S(1)} %get-tuple-element.41.weights, ...), custom_call_target="tpu_custom_call" | custom-call | flops 256000000 | bytes 1048576 | tf_op jit(solution)/shard_map/pallas_call | solution.py:281
  21.8 2.5 %shard_map.64 = (bf16[128,8,256]{2,1,0:T(8,128)(2,1)S(1)}, bf16[128,8,256]{2,1,0:T(8,128)(2,1)S(1)}, bf16[128,8,256]{2,1,0:T(8,128)(2,1)S(1)}, bf16[128,8,256]{2,1,0:T(8,128)(2,1)S(1)}) custom-call(s32[4]{0:T(128)S(1)} %pad_add_fusion.1.here_ref, s32[512]{0:T(512)S(1)} %copy-done.1, bf16[16,256,256]{2,1,0:T(8,128)(2,1)S(1)} %get-tuple-element.41.weights, ...), custom_call_target="tpu_custom_call" | custom-call | flops 256000000 | bytes 1048576 | tf_op jit(solution)/shard_map/pallas_call | solution.py:281
  24.3 6.0 %collective-permute-done.3.b_ref = bf16[128,8,512]{2,1,0:T(8,128)(2,1)S(1)} collective-permute-done((bf16[128,8,512]{2,1,0:T(8,128)(2,1)S(1)}, bf16[128,8,512]{2,1,0:T(8,128)(2,1)S(1)}, u32[]{:S(2)}, u32[]{:S(2)}) %collective-permute-start.3) | collective-permute-done | bytes 1048608 | tf_op jit(solution)/shard_map/ppermute | solution.py:48
  32.5 3.8 %collective-permute-done.8.b_ref = bf16[128,8,256]{2,1,0:T(8,128)(2,1)S(1)} collective-permute-done((bf16[128,8,256]{2,1,0:T(8,128)(2,1)S(1)}, bf16[128,8,256]{2,1,0:T(8,128)(2,1)S(1)}, u32[]{:S(2)}, u32[]{:S(2)}) %collective-permute-start.8) | collective-permute-done | bytes 524320 | tf_op jit(solution)/shard_map/ppermute | solution.py:48
  36.4 2.9 %collective-permute-start.9 = (bf16[128,8,256]{2,1,0:T(8,128)(2,1)S(1)}, bf16[128,8,256]{2,1,0:T(8,128)(2,1)S(1)}, u32[]{:S(2)}, u32[]{:S(2)}) collective-permute-start(bf16[128,8,256]{2,1,0:T(8,128)(2,1)S(1)} %shard_map.66), channel_id=1, source_target_pairs={{0,96},{1,97},{2,26},{3,27},{4,100},{5,101},{6,30},{7,31},{8,104},... | collective-permute-start | bytes 1572872 | tf_op jit(solution)/shard_map/ppermute | solution.py:48
  39.3 4.0 %collective-permute-start.13 = (bf16[128,8,256]{2,1,0:T(8,128)(2,1)S(1)}, bf16[128,8,256]{2,1,0:T(8,128)(2,1)S(1)}, u32[]{:S(2)}, u32[]{:S(2)}) collective-permute-start(bf16[128,8,256]{2,1,0:T(8,128)(2,1)S(1)} %get-tuple-element.58), channel_id=1, source_target_pairs={{0,1},{1,0},{2,3},{3,2},{4,5},{5,4},{6,7},{7,6},{8,9},{9,8},{10,11... | collective-permute-start | bytes 1572872 | tf_op jit(solution)/shard_map/ppermute | solution.py:48
  43.3 8.9 %collective-permute-done.7.refs_4_ = bf16[128,8,256]{2,1,0:T(8,128)(2,1)S(1)} collective-permute-done((bf16[128,8,256]{2,1,0:T(8,128)(2,1)S(1)}, bf16[128,8,256]{2,1,0:T(8,128)(2,1)S(1)}, u32[]{:S(2)}, u32[]{:S(2)}) %collective-permute-start.7) | collective-permute-done | bytes 524320 | tf_op jit(solution)/shard_map/ppermute | solution.py:48
  52.2 2.0 %collective-permute-start.14 = (bf16[128,8,256]{2,1,0:T(8,128)(2,1)S(1)}, bf16[128,8,256]{2,1,0:T(8,128)(2,1)S(1)}, u32[]{:S(2)}, u32[]{:S(2)}) collective-permute-start(bf16[128,8,256]{2,1,0:T(8,128)(2,1)S(1)} %get-tuple-element.59), channel_id=1, source_target_pairs={{0,4},{1,5},{2,6},{3,7},{4,1},{5,0},{6,3},{7,2},{8,12},{9,13},{10,... | collective-permute-start | bytes 1572872 | tf_op jit(solution)/shard_map/ppermute | solution.py:48
  54.3 2.1 %collective-permute-start.15 = (bf16[128,8,256]{2,1,0:T(8,128)(2,1)S(1)}, bf16[128,8,256]{2,1,0:T(8,128)(2,1)S(1)}, u32[]{:S(2)}, u32[]{:S(2)}) collective-permute-start(bf16[128,8,256]{2,1,0:T(8,128)(2,1)S(1)} %get-tuple-element.60), channel_id=1, source_target_pairs={{0,5},{1,4},{2,7},{3,6},{4,0},{5,1},{6,2},{7,3},{8,13},{9,12},{10,... | collective-permute-start | bytes 1572872 | tf_op jit(solution)/shard_map/ppermute | solution.py:48
  57.4 3.2 %collective-permute-start.10 = (bf16[32,8,768]{2,1,0:T(8,128)(2,1)S(1)}, bf16[32,8,768]{2,1,0:T(8,128)(2,1)S(1)}, u32[]{:S(2)}, u32[]{:S(2)}) collective-permute-start(bf16[32,8,768]{2,1,0:T(8,128)(2,1)S(1)} %get-tuple-element.55), channel_id=1, source_target_pairs={{0,16},{1,17},{2,3},{3,2},{4,20},{5,21},{6,7},{7,6},{8,24},{9,25},... | collective-permute-start | bytes 1179656 | tf_op jit(solution)/shard_map/ppermute | solution.py:48
  61.3 2.6 %collective-permute-start.12 = (bf16[32,8,768]{2,1,0:T(8,128)(2,1)S(1)}, bf16[32,8,768]{2,1,0:T(8,128)(2,1)S(1)}, u32[]{:S(2)}, u32[]{:S(2)}) collective-permute-start(bf16[32,8,768]{2,1,0:T(8,128)(2,1)S(1)} %get-tuple-element.57), channel_id=1, source_target_pairs={{0,24},{1,25},{2,7},{3,6},{4,28},{5,29},{6,2},{7,3},{8,0},{9,1},{1... | collective-permute-start | bytes 1179656 | tf_op jit(solution)/shard_map/ppermute | solution.py:48
  63.9 9.5 %collective-permute-done.14.refs_2_ = bf16[128,8,256]{2,1,0:T(8,128)(2,1)S(1)} collective-permute-done((bf16[128,8,256]{2,1,0:T(8,128)(2,1)S(1)}, bf16[128,8,256]{2,1,0:T(8,128)(2,1)S(1)}, u32[]{:S(2)}, u32[]{:S(2)}) %collective-permute-start.14) | collective-permute-done | bytes 524320 | tf_op jit(solution)/shard_map/ppermute | solution.py:48
  74.9 2.5 %collective-permute-start.21 = (bf16[32,8,256]{2,1,0:T(8,128)(2,1)S(1)}, bf16[32,8,256]{2,1,0:T(8,128)(2,1)S(1)}, u32[]{:S(2)}, u32[]{:S(2)}) collective-permute-start(bf16[32,8,256]{2,1,0:T(8,128)(2,1)S(1)} %get-tuple-element.68), channel_id=1, source_target_pairs={{0,96},{1,97},{2,98},{3,99},{4,100},{5,101},{6,102},{7,103},{8,104... | collective-permute-start | bytes 393224 | tf_op jit(solution)/shard_map/ppermute | solution.py:48
  77.6 3.4 %collective-permute-done.19.refs_1_ = bf16[32,8,256]{2,1,0:T(8,128)(2,1)S(1)} collective-permute-done((bf16[32,8,256]{2,1,0:T(8,128)(2,1)}, bf16[32,8,256]{2,1,0:T(8,128)(2,1)S(1)}, u32[]{:S(2)}, u32[]{:S(2)}) %collective-permute-start.19) | collective-permute-done | bytes 131104 | tf_op jit(solution)/shard_map/ppermute | solution.py:48
  81.8 2.7 %collective-permute-start.22 = (bf16[8,8,256]{2,1,0:T(8,128)(2,1)S(1)}, bf16[8,8,256]{2,1,0:T(8,128)(2,1)S(1)}, u32[]{:S(2)}, u32[]{:S(2)}) collective-permute-start(bf16[8,8,256]{2,1,0:T(8,128)(2,1)S(1)} %get-tuple-element.70), channel_id=1, source_target_pairs={{0,8},{1,9},{2,10},{3,11},{4,12},{5,13},{6,14},{7,15},{8,16},{9,17... | collective-permute-start | bytes 98312 | tf_op jit(solution)/shard_map/ppermute | solution.py:48
  85.9 2.0 %collective-permute-start.17 = (bf16[8,8,768]{2,1,0:T(8,128)(2,1)S(1)}, bf16[8,8,768]{2,1,0:T(8,128)(2,1)S(1)}, u32[]{:S(2)}, u32[]{:S(2)}) collective-permute-start(bf16[8,8,768]{2,1,0:T(8,128)(2,1)S(1)} %get-tuple-element.64), channel_id=1, source_target_pairs={{0,5},{1,4},{2,98},{3,99},{4,0},{5,1},{6,102},{7,103},{8,13},{9,12... | collective-permute-start | bytes 294920 | tf_op jit(solution)/shard_map/ppermute | solution.py:48
  90.6 2.5 %collective-permute-start.24 = (bf16[8,8,256]{2,1,0:T(8,128)(2,1)S(1)}, bf16[8,8,256]{2,1,0:T(8,128)(2,1)S(1)}, u32[]{:S(2)}, u32[]{:S(2)}) collective-permute-start(bf16[8,8,256]{2,1,0:T(8,128)(2,1)S(1)} %get-tuple-element.72), channel_id=1, source_target_pairs={{0,16},{1,17},{2,18},{3,19},{4,20},{5,21},{6,22},{7,23},{8,24},{9,... | collective-permute-start | bytes 98312 | tf_op jit(solution)/shard_map/ppermute | solution.py:48
  93.2 2.9 %collective-permute-done.24.refs_7_ = bf16[8,8,256]{2,1,0:T(8,128)(2,1)S(1)} collective-permute-done((bf16[8,8,256]{2,1,0:T(8,128)(2,1)S(1)}, bf16[8,8,256]{2,1,0:T(8,128)(2,1)S(1)}, u32[]{:S(2)}, u32[]{:S(2)}) %collective-permute-start.24) | collective-permute-done | bytes 32800 | tf_op jit(solution)/shard_map/ppermute | solution.py:48
  98.0 8.6 %all-to-all-start = ((f32[128,1,160]{2,1,0:T(1,128)}), f32[128,1,160]{2,1,0:T(1,128)S(1)}, u32[]{:S(2)}, u32[]{:S(2)}) async-start(f32[128,1,160]{2,1,0:T(1,128)} %copy.8), calls=%async_computation | async-start | bytes 262144 | tf_op jit(solution)/shard_map/all_to_all | solution.py:445
  106.7 9.1 %all-to-all-done = f32[128,1,160]{2,1,0:T(1,128)S(1)} async-done(((f32[128,1,160]{2,1,0:T(1,128)}), f32[128,1,160]{2,1,0:T(1,128)S(1)}, u32[]{:S(2)}, u32[]{:S(2)}) %all-to-all-start) | async-done | bytes 81952 | tf_op jit(solution)/shard_map/all_to_all | solution.py:445
  (60 shorter events, 22.1 us)
Async XLA Ops:
  5.0 6.8 %collective-permute-start.1 = (bf16[4,512,512]{2,1,0:T(8,128)(2,1)}, bf16[4,512,512]{2,1,0:T(8,128)(2,1)S(1)}, u32[]{:S(2)}, u32[]{:S(2)}) collective-permute-start(bf16[4,512,512]{2,1,0:T(8,128)(2,1)} %get-tuple-element.43), channel_id=1, source_target_pairs={{0,2},{2,0},{1,3},{3,1},{4,6},{6,4},{5,7},{7,5},{8,10},{10,8},{9,1... | collective-permute-start | bytes 6291464 | tf_op jit(solution)/shard_map/ppermute | solution.py:52
  5.6 16.1 %collective-permute-start.4 = (bf16[4,512,256]{2,1,0:T(8,128)(2,1)}, bf16[4,512,256]{2,1,0:T(8,128)(2,1)}, u32[]{:S(2)}, u32[]{:S(2)}) collective-permute-start(bf16[4,512,256]{2,1,0:T(8,128)(2,1)} %get-tuple-element.48), channel_id=1, source_target_pairs={{0,2},{2,0},{1,3},{3,1},{4,6},{6,4},{5,7},{7,5},{8,10},{10,8},{9,1... | collective-permute-start | bytes 3145736 | tf_op jit(solution)/shard_map/ppermute | solution.py:52
  7.0 10.6 %collective-permute-start.5 = (bf16[4,512,256]{2,1,0:T(8,128)(2,1)S(1)}, bf16[4,512,256]{2,1,0:T(8,128)(2,1)}, u32[]{:S(2)}, u32[]{:S(2)}) collective-permute-start(bf16[4,512,256]{2,1,0:T(8,128)(2,1)S(1)} %shard_map.60.rest_0_), channel_id=1, source_target_pairs={{0,2},{2,0},{1,3},{3,1},{4,6},{6,4},{5,7},{7,5},{8,10},{10,8},{9,1... | collective-permute-start | bytes 3145736 | tf_op jit(solution)/shard_map/ppermute | solution.py:52
  14.2 16.1 %collective-permute-start.3 = (bf16[128,8,512]{2,1,0:T(8,128)(2,1)S(1)}, bf16[128,8,512]{2,1,0:T(8,128)(2,1)S(1)}, u32[]{:S(2)}, u32[]{:S(2)}) collective-permute-start(bf16[128,8,512]{2,1,0:T(8,128)(2,1)S(1)} %get-tuple-element.47), channel_id=1, source_target_pairs={{0,32},{1,33},{2,10},{3,11},{4,36},{5,37},{6,14},{7,15},{8,40},{9,... | collective-permute-start | bytes 3145736 | tf_op jit(solution)/shard_map/ppermute | solution.py:48
  15.9 38.4 %collective-permute-start.2 = (bf16[128,8,512]{2,1,0:T(8,128)(2,1)S(1)}, bf16[128,8,512]{2,1,0:T(8,128)(2,1)S(1)}, u32[]{:S(2)}, u32[]{:S(2)}) collective-permute-start(bf16[128,8,512]{2,1,0:T(8,128)(2,1)S(1)} %get-tuple-element.45), channel_id=1, source_target_pairs={{0,96},{1,97},{2,26},{3,27},{4,100},{5,101},{6,30},{7,31},{8,104},... | collective-permute-start | bytes 3145736 | tf_op jit(solution)/shard_map/ppermute | solution.py:48
  20.0 16.3 %collective-permute-start.8 = (bf16[128,8,256]{2,1,0:T(8,128)(2,1)S(1)}, bf16[128,8,256]{2,1,0:T(8,128)(2,1)S(1)}, u32[]{:S(2)}, u32[]{:S(2)}) collective-permute-start(bf16[128,8,256]{2,1,0:T(8,128)(2,1)S(1)} %get-tuple-element.53), channel_id=1, source_target_pairs={{0,96},{1,97},{2,26},{3,27},{4,100},{5,101},{6,30},{7,31},{8,104},... | collective-permute-start | bytes 1572872 | tf_op jit(solution)/shard_map/ppermute | solution.py:48
  30.5 25.9 %collective-permute-start.6 = (bf16[128,8,512]{2,1,0:T(8,128)(2,1)S(1)}, bf16[128,8,512]{2,1,0:T(8,128)(2,1)S(1)}, u32[]{:S(2)}, u32[]{:S(2)}) collective-permute-start(bf16[128,8,512]{2,1,0:T(8,128)(2,1)S(1)} %shard_map.65.rest_0_), channel_id=1, source_target_pairs={{0,32},{1,33},{2,10},{3,11},{4,36},{5,37},{6,14},{7,15},{8,40},{9,... | collective-permute-start | bytes 3145736 | tf_op jit(solution)/shard_map/ppermute | solution.py:48
  31.0 21.2 %collective-permute-start.7 = (bf16[128,8,256]{2,1,0:T(8,128)(2,1)S(1)}, bf16[128,8,256]{2,1,0:T(8,128)(2,1)S(1)}, u32[]{:S(2)}, u32[]{:S(2)}) collective-permute-start(bf16[128,8,256]{2,1,0:T(8,128)(2,1)S(1)} %get-tuple-element.51), channel_id=1, source_target_pairs={{0,32},{1,33},{2,10},{3,11},{4,36},{5,37},{6,14},{7,15},{8,40},{9,... | collective-permute-start | bytes 1572872 | tf_op jit(solution)/shard_map/ppermute | solution.py:48
  36.4 20.0 %collective-permute-start.9 = (bf16[128,8,256]{2,1,0:T(8,128)(2,1)S(1)}, bf16[128,8,256]{2,1,0:T(8,128)(2,1)S(1)}, u32[]{:S(2)}, u32[]{:S(2)}) collective-permute-start(bf16[128,8,256]{2,1,0:T(8,128)(2,1)S(1)} %shard_map.66), channel_id=1, source_target_pairs={{0,96},{1,97},{2,26},{3,27},{4,100},{5,101},{6,30},{7,31},{8,104},... | collective-permute-start | bytes 1572872 | tf_op jit(solution)/shard_map/ppermute | solution.py:48
  39.3 22.0 %collective-permute-start.13 = (bf16[128,8,256]{2,1,0:T(8,128)(2,1)S(1)}, bf16[128,8,256]{2,1,0:T(8,128)(2,1)S(1)}, u32[]{:S(2)}, u32[]{:S(2)}) collective-permute-start(bf16[128,8,256]{2,1,0:T(8,128)(2,1)S(1)} %get-tuple-element.58), channel_id=1, source_target_pairs={{0,1},{1,0},{2,3},{3,2},{4,5},{5,4},{6,7},{7,6},{8,9},{9,8},{10,11... | collective-permute-start | bytes 1572872 | tf_op jit(solution)/shard_map/ppermute | solution.py:48
  52.2 21.1 %collective-permute-start.14 = (bf16[128,8,256]{2,1,0:T(8,128)(2,1)S(1)}, bf16[128,8,256]{2,1,0:T(8,128)(2,1)S(1)}, u32[]{:S(2)}, u32[]{:S(2)}) collective-permute-start(bf16[128,8,256]{2,1,0:T(8,128)(2,1)S(1)} %get-tuple-element.59), channel_id=1, source_target_pairs={{0,4},{1,5},{2,6},{3,7},{4,1},{5,0},{6,3},{7,2},{8,12},{9,13},{10,... | collective-permute-start | bytes 1572872 | tf_op jit(solution)/shard_map/ppermute | solution.py:48
  54.3 19.1 %collective-permute-start.15 = (bf16[128,8,256]{2,1,0:T(8,128)(2,1)S(1)}, bf16[128,8,256]{2,1,0:T(8,128)(2,1)S(1)}, u32[]{:S(2)}, u32[]{:S(2)}) collective-permute-start(bf16[128,8,256]{2,1,0:T(8,128)(2,1)S(1)} %get-tuple-element.60), channel_id=1, source_target_pairs={{0,5},{1,4},{2,7},{3,6},{4,0},{5,1},{6,2},{7,3},{8,13},{9,12},{10,... | collective-permute-start | bytes 1572872 | tf_op jit(solution)/shard_map/ppermute | solution.py:48
  57.4 17.4 %collective-permute-start.10 = (bf16[32,8,768]{2,1,0:T(8,128)(2,1)S(1)}, bf16[32,8,768]{2,1,0:T(8,128)(2,1)S(1)}, u32[]{:S(2)}, u32[]{:S(2)}) collective-permute-start(bf16[32,8,768]{2,1,0:T(8,128)(2,1)S(1)} %get-tuple-element.55), channel_id=1, source_target_pairs={{0,16},{1,17},{2,3},{3,2},{4,20},{5,21},{6,7},{7,6},{8,24},{9,25},... | collective-permute-start | bytes 1179656 | tf_op jit(solution)/shard_map/ppermute | solution.py:48
  60.6 16.8 %collective-permute-start.11 = (bf16[32,8,768]{2,1,0:T(8,128)(2,1)}, bf16[32,8,768]{2,1,0:T(8,128)(2,1)S(1)}, u32[]{:S(2)}, u32[]{:S(2)}) collective-permute-start(bf16[32,8,768]{2,1,0:T(8,128)(2,1)} %get-tuple-element.56), channel_id=1, source_target_pairs={{0,8},{1,9},{2,6},{3,7},{4,12},{5,13},{6,3},{7,2},{8,16},{9,17},{1... | collective-permute-start | bytes 1179656 | tf_op jit(solution)/shard_map/ppermute | solution.py:48
  61.3 16.1 %collective-permute-start.12 = (bf16[32,8,768]{2,1,0:T(8,128)(2,1)S(1)}, bf16[32,8,768]{2,1,0:T(8,128)(2,1)S(1)}, u32[]{:S(2)}, u32[]{:S(2)}) collective-permute-start(bf16[32,8,768]{2,1,0:T(8,128)(2,1)S(1)} %get-tuple-element.57), channel_id=1, source_target_pairs={{0,24},{1,25},{2,7},{3,6},{4,28},{5,29},{6,2},{7,3},{8,0},{9,1},{1... | collective-permute-start | bytes 1179656 | tf_op jit(solution)/shard_map/ppermute | solution.py:48
  74.1 6.8 %collective-permute-start.19 = (bf16[32,8,256]{2,1,0:T(8,128)(2,1)}, bf16[32,8,256]{2,1,0:T(8,128)(2,1)S(1)}, u32[]{:S(2)}, u32[]{:S(2)}) collective-permute-start(bf16[32,8,256]{2,1,0:T(8,128)(2,1)} %get-tuple-element.66), channel_id=1, source_target_pairs={{0,64},{1,65},{2,66},{3,67},{4,68},{5,69},{6,70},{7,71},{8,72},{9,... | collective-permute-start | bytes 393224 | tf_op jit(solution)/shard_map/ppermute | solution.py:48
  74.1 7.6 %collective-permute-start.20 = (bf16[32,8,256]{2,1,0:T(8,128)(2,1)S(1)}, bf16[32,8,256]{2,1,0:T(8,128)(2,1)S(1)}, u32[]{:S(2)}, u32[]{:S(2)}) collective-permute-start(bf16[32,8,256]{2,1,0:T(8,128)(2,1)S(1)} %get-tuple-element.67), channel_id=1, source_target_pairs={{0,32},{1,33},{2,34},{3,35},{4,36},{5,37},{6,38},{7,39},{8,40},{9,... | collective-permute-start | bytes 393224 | tf_op jit(solution)/shard_map/ppermute | solution.py:48
  74.9 6.9 %collective-permute-start.21 = (bf16[32,8,256]{2,1,0:T(8,128)(2,1)S(1)}, bf16[32,8,256]{2,1,0:T(8,128)(2,1)S(1)}, u32[]{:S(2)}, u32[]{:S(2)}) collective-permute-start(bf16[32,8,256]{2,1,0:T(8,128)(2,1)S(1)} %get-tuple-element.68), channel_id=1, source_target_pairs={{0,96},{1,97},{2,98},{3,99},{4,100},{5,101},{6,102},{7,103},{8,104... | collective-permute-start | bytes 393224 | tf_op jit(solution)/shard_map/ppermute | solution.py:48
  81.8 8.8 %collective-permute-start.22 = (bf16[8,8,256]{2,1,0:T(8,128)(2,1)S(1)}, bf16[8,8,256]{2,1,0:T(8,128)(2,1)S(1)}, u32[]{:S(2)}, u32[]{:S(2)}) collective-permute-start(bf16[8,8,256]{2,1,0:T(8,128)(2,1)S(1)} %get-tuple-element.70), channel_id=1, source_target_pairs={{0,8},{1,9},{2,10},{3,11},{4,12},{5,13},{6,14},{7,15},{8,16},{9,17... | collective-permute-start | bytes 98312 | tf_op jit(solution)/shard_map/ppermute | solution.py:48
  84.6 11.4 %collective-permute-start.16 = (bf16[8,8,768]{2,1,0:T(8,128)(2,1)S(1)}, bf16[8,8,768]{2,1,0:T(8,128)(2,1)S(1)}, u32[]{:S(2)}, u32[]{:S(2)}) collective-permute-start(bf16[8,8,768]{2,1,0:T(8,128)(2,1)S(1)} %get-tuple-element.63), channel_id=1, source_target_pairs={{0,4},{1,5},{2,34},{3,35},{4,1},{5,0},{6,38},{7,39},{8,12},{9,13},... | collective-permute-start | bytes 294920 | tf_op jit(solution)/shard_map/ppermute | solution.py:48
  85.9 10.2 %collective-permute-start.17 = (bf16[8,8,768]{2,1,0:T(8,128)(2,1)S(1)}, bf16[8,8,768]{2,1,0:T(8,128)(2,1)S(1)}, u32[]{:S(2)}, u32[]{:S(2)}) collective-permute-start(bf16[8,8,768]{2,1,0:T(8,128)(2,1)S(1)} %get-tuple-element.64), channel_id=1, source_target_pairs={{0,5},{1,4},{2,98},{3,99},{4,0},{5,1},{6,102},{7,103},{8,13},{9,12... | collective-permute-start | bytes 294920 | tf_op jit(solution)/shard_map/ppermute | solution.py:48
  87.8 8.2 %collective-permute-start.18 = (bf16[8,8,768]{2,1,0:T(8,128)(2,1)S(1)}, bf16[8,8,768]{2,1,0:T(8,128)(2,1)S(1)}, u32[]{:S(2)}, u32[]{:S(2)}) collective-permute-start(bf16[8,8,768]{2,1,0:T(8,128)(2,1)S(1)} %get-tuple-element.65), channel_id=1, source_target_pairs={{0,1},{1,0},{2,66},{3,67},{4,5},{5,4},{6,70},{7,71},{8,9},{9,8},{1... | collective-permute-start | bytes 294920 | tf_op jit(solution)/shard_map/ppermute | solution.py:48
  98.0 17.8 %all-to-all-start = ((f32[128,1,160]{2,1,0:T(1,128)}), f32[128,1,160]{2,1,0:T(1,128)S(1)}, u32[]{:S(2)}, u32[]{:S(2)}) async-start(f32[128,1,160]{2,1,0:T(1,128)} %copy.8), calls=%async_computation | async-start | bytes 262144 | tf_op jit(solution)/shard_map/all_to_all | solution.py:445
  106.6 10.1 %collective-permute-start.25 = (f32[4,8,1024]{2,1,0:T(8,128)S(1)}, f32[4,8,1024]{2,1,0:T(8,128)S(1)}, u32[]{:S(2)}, u32[]{:S(2)}) collective-permute-start(f32[4,8,1024]{2,1,0:T(8,128)S(1)} %get-tuple-element.74), channel_id=1, source_target_pairs={{0,2},{2,0},{1,3},{3,1},{4,6},{6,4},{5,7},{7,5},{8,10},{10,8},{9,1... | collective-permute-start | bytes 393224 | tf_op jit(solution)/shard_map/ppermute | solution.py:52
  (5 other events, 20.2 us)
